TPU v7x, 32 devices: a whole 2x2x4 slice. The times are simulated.
32 devices in a mesh: row: 8 (over z, y), col: 4 (over x, core).
Axes of the slice: x: 2, y: 2, z: 4, core: 2. Of those that a mesh axis runs over, the one named last changes fastest.
Arguments:
- embeddings: bfloat16 [12288, 768], P(('row', 'col'))
- doc_order: int32 [12288], P(('row', 'col')), may hold values from 0 to 12287, each once
Outputs:
- nearest_earlier: float32 [12288], P(('row', 'col'))
Inputs may be any that keep to these rules, and one draw needn't show every extreme that they name: `doc_order`: each value 0 to 12287 appears once.
All inputs are finite; a program needn't handle non-finite values.
Results may differ from a plain program's by a relative error of at most 0.00051.
Values may be sent and summed in bfloat16 or wider, within the bound.
A program may use at most 64 MiB of HBM per device.

v0:
```python
import functools

import jax
import jax.numpy as jnp
from jax import lax
from jax.experimental import pallas as pl
from jax.experimental.pallas import tpu as pltpu
from jax.sharding import PartitionSpec as P

MESH = pl.DeviceIdType.MESH
LANES = 128
PIECE = 64
GROUP = 128


def fast_size(rows):
    best = 1
    for size in range(1, rows + 1):
        if rows % size == 0 and size * size <= rows:
            best = size
    return best


class Layout:
    def __init__(self, rows, cols):
        self.fast = fast_size(rows)
        self.slow = rows // self.fast
        self.cores = 2 if cols % 2 == 0 else 1
        self.xs = cols // self.cores
        self.chips = self.fast * self.xs
        self.plane = self.chips * self.cores
        self.top = self.slow - 2 if self.slow > 2 else self.slow - 1
        self.down = self.slow > 2
        chips = [(f, x) for f in range(self.fast) for x in range(self.xs)]
        near = [c for c in chips if (c[0] == 0) != (c[1] == 0)]
        far = [c for c in chips if c[0] != 0 and c[1] != 0]
        self.offsets = near + far
        self.near = list(range(len(near)))
        self.far = list(range(len(near), len(near) + len(far)))
        self.peers = [
            (f, x, c)
            for f in range(self.fast)
            for x in range(self.xs)
            for c in range(self.cores)
            if (f, x, c) != (0, 0, 0)
        ]


def kernel(
    lay, n, chunks,
    emb, order, out,
    units, line, orders, line_orders, col_orders,
    row_best, col_best, plane_res, line_res, plane_in, line_in, line_best,
    ps, pr, ss, sr, ls, lr, os_, or_, los, lor, oss, osr, rs, rr, lrs, lrr,
):
    S, F, X, C = lay.slow, lay.fast, lay.xs, lay.cores
    rows_here = n // chunks
    align = PIECE if rows_here % PIECE == 0 else rows_here
    r, c = lax.axis_index("row"), lax.axis_index("col")
    z, f = r // F, lax.rem(r, F)
    x, core = c // C, lax.rem(c, C)
    chip = f * X + x
    slot = chip * C + core

    def plane_id(df, dx, dc):
        return {
            "row": z * F + lax.rem(f + df, F),
            "col": lax.rem(x + dx, X) * C + lax.rem(core + dc, C),
        }

    def line_id(there):
        return {"row": there * F + f, "col": c}

    def source_chip(df, dx):
        return lax.rem(f + F - df, F) * X + lax.rem(x + X - dx, X)

    def span(which, k):
        return pl.ds(pl.multiple_of(which * n + k * rows_here, align), rows_here)

    def remote(src, dst, send, recv, where):
        return pltpu.make_async_remote_copy(
            src_ref=src, dst_ref=dst, send_sem=send, recv_sem=recv,
            device_id=where, device_id_type=MESH,
        )

    def plane_copy(i, k):
        part = units.at[span(slot, k)]
        return remote(part, part, ps.at[i, k], pr.at[i, k], plane_id(*lay.offsets[i], 0))

    def relay_copy(i, k):
        df, dx = lay.offsets[i]
        src, step = ((0, dx), (df, 0)) if k % 2 == 0 else ((df, 0), (0, dx))
        part = units.at[span(source_chip(*src) * C + core, k)]
        return remote(part, part, ps.at[i, k], pr.at[i, k], plane_id(*step, 0))

    def sibling_copy(i, k):
        src = chip if i < 0 else source_chip(*lay.offsets[i])
        part = units.at[span(src * C + core, k)]
        return remote(part, part, ss.at[i + 1, k], sr.at[i + 1, k], plane_id(0, 0, 1))

    def plane_wait(i, k):
        src = source_chip(*lay.offsets[i]) * C + core
        part = units.at[span(src, k)]
        remote(part, part, ps.at[i, k], pr.at[i, k], plane_id(*lay.offsets[i], 0)).wait_recv()

    def sibling_wait(i, k):
        src = chip if i < 0 else source_chip(*lay.offsets[i])
        part = units.at[span(src * C + lax.rem(core + 1, C), k)]
        remote(part, part, ss.at[i + 1, k], sr.at[i + 1, k], plane_id(0, 0, 1)).wait_recv()

    def line_copy(src, k, dst_slot, tag, there):
        return remote(
            src, line.at[dst_slot, pl.ds(k * rows_here, rows_here)],
            ls.at[tag, k], lr.at[dst_slot, k], line_id(there),
        )

    def own_part(k):
        return units.at[span(slot, k)]

    base = jnp.minimum(z, lay.top)
    sends_up = z < lay.top
    last = S - 1
    sends_down = (z == last) if lay.down else None
    takes_down = (z == last - 1) if lay.down else None

    def relays(w, k):
        part = line.at[w, pl.ds(k * rows_here, rows_here)]
        found = []
        if w < lay.top:
            found.append(((base >= w) & (z < lay.top), line_copy(part, k, w + 1, w, z + 1)))
        if lay.down:
            found.append(((base >= w) & (z == lay.top), line_copy(part, k, w, w, z + 1)))
        return found

    def order_send(src, i, where):
        return remote(orders.at[src], orders.at[src], os_.at[i], or_.at[i], where)

    def order_copy(i):
        return order_send(slot, i, plane_id(*lay.offsets[i], 0))

    def order_relay(i):
        df, dx = lay.offsets[i]
        return order_send(source_chip(0, dx) * C + core, i, plane_id(df, 0, 0))

    def order_wait(i):
        order_send(source_chip(*lay.offsets[i]) * C + core, i, plane_id(0, 0, 1)).wait_recv()

    def order_across(i, side):
        src = chip if i < 0 else source_chip(*lay.offsets[i])
        part = orders.at[src * C + lax.rem(core + side, C)]
        return remote(part, part, oss.at[i + 1], osr.at[i + 1], plane_id(0, 0, 1))

    def meets(src, dst):
        up = (src < dst) & ((src != lay.top) | (not lay.down))
        if lay.down:
            up = up | ((src == last) & (dst == last - 1))
        return up

    def line_order_copy(part, src, tag, there):
        return remote(part, line_orders.at[src], los.at[tag], lor.at[src], line_id(there))

    def own_order(there):
        return line_order_copy(orders.at[slot], z, 0, there)

    def order_up(w):
        return line_order_copy(line_orders.at[base - w], base - w, w, z + 1)

    def goes_on(w):
        return (base >= w) & (z < last) & (lay.down | (z < lay.top))

    barrier = pltpu.get_barrier_semaphore()
    steps = [(*lay.offsets[i], 0) for i in lay.near] + ([(0, 0, 1)] if C > 1 else [])
    sides = ((z > 0, z - 1), (z < last, z + 1))
    for step in steps:
        pl.semaphore_signal(barrier, inc=1, device_id=plane_id(*step), device_id_type=MESH)
    for there, which in sides:
        pl.when(there)(
            lambda which=which: pl.semaphore_signal(
                barrier, inc=1, device_id=line_id(which), device_id_type=MESH
            )
        )

    orders[pl.ds(slot, 1)] = order[...].reshape(1, 1, n)

    def spread(which, row):
        wide = jnp.broadcast_to(row.reshape(1, n), (LANES, n))
        col_orders[which] = wide.T

    def normalize(k):
        floats = emb[pl.ds(k * rows_here, rows_here), :].astype(jnp.float32)
        scale = lax.rsqrt(jnp.sum(floats * floats, axis=1, keepdims=True) + 1e-06)
        units[span(slot, k), :] = (floats * scale).astype(jnp.bfloat16)

    def send_own(k):
        pl.when(sends_up)(lambda: line_copy(own_part(k), k, 1, lay.top + 1, z + 1).start())
        if lay.down:
            pl.when(sends_down)(lambda: line_copy(own_part(k), k, 0, 0, z - 1).start())
        for i in lay.near:
            plane_copy(i, k).start()
        if C > 1:
            sibling_copy(-1, k).start()

    for k in range(chunks):
        normalize(k)
    lines = jnp.minimum(z, 1) + jnp.minimum(last - z, 1)
    pl.semaphore_wait(barrier, len(steps) + lines)
    pl.when(sends_up)(lambda: own_order(z + 1).start())
    if lay.down:
        pl.when(sends_down)(lambda: own_order(z - 1).start())
    for i in lay.near:
        order_copy(i).start()
    if C > 1:
        order_across(-1, 0).start()
    for k in range(chunks):
        send_own(k)

    row_best[...] = jnp.full(row_best.shape, -1.0, jnp.float32)
    col_best[...] = jnp.full(col_best.shape, -1.0, jnp.float32)
    spread(lay.top + 1, order[...].reshape(1, n))

    width = C * n

    def item(lhs, w, first_chip, both, first=0, count=n, wide=1):
        rhs = units[pl.ds(pl.multiple_of(first_chip * width, LANES), wide * width), :]
        s = lax.dot_general(
            lhs, rhs, (((1,), (1,)), ((), ())), preferred_element_type=jnp.float32
        )
        mine = col_orders[w, first:first + count, :]
        rows_max = None
        for j in range(wide * width // LANES):
            part = s[:, j * LANES:(j + 1) * LANES]
            which_chip, at = first_chip + j * LANES // width, j * LANES % width
            core_at, lane_at = at // n, at % n
            theirs = orders[which_chip * C + core_at, :, lane_at:lane_at + LANES]
            earlier = theirs < mine
            if both:
                cand = jnp.where(earlier, part, jnp.float32(-1.0))
                rows_max = cand if rows_max is None else jnp.maximum(rows_max, cand)
                later = jnp.where(earlier, jnp.float32(-1.0), part)
            else:
                later = jnp.where(mine < theirs, part, jnp.float32(-1.0))
            down = jnp.max(later.reshape(count // 8, 8, LANES), axis=0)
            col_best[which_chip, :, at:at + LANES] = jnp.maximum(
                col_best[which_chip, :, at:at + LANES], down
            )
        if both:
            row_best[w, first:first + count, :] = jnp.maximum(
                row_best[w, first:first + count, :], rows_max
            )

    def own_item(which_chip):
        lhs = units[pl.ds(pl.multiple_of(slot * n, LANES), n), :]
        item(lhs, lay.top + 1, which_chip, False)

    def line_item(w, which_chip):
        item(line[w], w, which_chip, True)

    def valid(w):
        return takes_down if w == 0 else base >= w

    early = [w for w in ([0] if lay.down else []) + [1] if w <= lay.top]
    late = list(range(2, lay.top + 1))

    def take_order(w):
        src = (z + 1) if w == 0 else base - w
        line_order_copy(line_orders.at[src], src, 0, z).wait_recv()
        if w > 0:
            pl.when(goes_on(w))(lambda: order_up(w).start())
        spread(w, line_orders[src])

    for i in lay.near:
        order_wait(i)
        if C > 1:
            order_across(i, 0).start()
    for i in lay.far:
        order_relay(i).start()
    if C > 1:
        order_across(-1, 1).wait_recv()
        for k in range(chunks):
            sibling_wait(-1, k)
    own_item(chip)
    if C > 1:
        for i in lay.near:
            order_across(i, 1).wait_recv()

    def line_wait(w, k):
        line_copy(line.at[w, pl.ds(k * rows_here, rows_here)], k, w, 0, z).wait_recv()

    def pass_on(w, k):
        if k == 0:
            pl.when(valid(w))(lambda: take_order(w))
        pl.when(valid(w))(lambda: line_wait(w, k))
        if w > 0:
            for cond, copy in relays(w, k):
                pl.when(cond)(lambda copy=copy: copy.start())

    def chips_of(places):
        def at(j):
            if places == "near":
                by_x = j < X - 1
                df = jnp.where(by_x, 0, j - (X - 2))
                dx = jnp.where(by_x, j + 1, 0)
            elif places == "far":
                df, dx = 1 + j // max(X - 1, 1), 1 + lax.rem(j, max(X - 1, 1))
            elif places == "self":
                df, dx = 0, 0
            else:
                df, dx = j // X, lax.rem(j, X)
            return source_chip(df, dx)

        count = {"near": F + X - 2, "far": (F - 1) * (X - 1), "self": 1, "all": F * X}
        return count[places], at

    def loop(places, body):
        count, at = chips_of(places)

        def step(j, carry):
            body(at(j))
            return carry

        if count:
            lax.fori_loop(0, count, step, 0)

    def own_sweep(places):
        loop(places, own_item)

    def line_sweep(w, places):
        pl.when(valid(w))(lambda: loop(places, lambda one: line_item(w, one)))

    wide = next(m for m in (4, 3, 2, 1) if lay.chips % m == 0)

    def late_sweep(w, first, count, here):
        def body(j, carry):
            item(line[w, first:first + count, :], w, j * wide, True, first, count, wide)
            return carry

        @pl.when(valid(w) & here)
        def run():
            lax.fori_loop(0, lay.chips // wide, body, 0)

    for k in range(chunks):
        for w in reversed(early):
            pass_on(w, k)
        for i in lay.near:
            plane_wait(i, k)
        for i in lay.far:
            relay_copy(i, k).start()
        if C > 1:
            for i in lay.near:
                sibling_copy(i, k).start()

    def line_result(w):
        there = z + 1 if w == 0 else base - w
        return remote(line_res.at[w], line_in.at[z], lrs.at[w], lrr.at[z], line_id(there))

    def give_back(w):
        @pl.when(valid(w))
        def fold():
            line_res[w] = jnp.max(row_best[w].T, axis=0, keepdims=True)
            line_result(w).start()

    def when_at(sixths):
        return min(chunks * sixths // 6, chunks - 1)

    plan = [[] for _ in range(chunks)]
    plan[when_at(0)].append(lambda: own_sweep("near"))
    for j, w in enumerate(reversed(early)):
        plan[when_at(1 + 2 * j)].append(lambda w=w: line_sweep(w, "near"))
        plan[when_at(2)].append(lambda w=w: line_sweep(w, "self"))
    plan[when_at(4)].append(lambda: own_sweep("far"))
    for j, w in enumerate(reversed(early)):
        plan[when_at(4 + j)].append(lambda w=w: line_sweep(w, "far"))
    split = n * 2 // 3 if chunks % 6 == 0 and n * 2 // 3 % GROUP == 0 else 0
    relaying = z == lay.top
    for w in reversed(early):
        plan[chunks - 1].append(lambda w=w: give_back(w))
    for w in late:
        if split:
            plan[(chunks * 2 + 2) // 3 - 1].append(
                lambda w=w: late_sweep(w, 0, split, jnp.logical_not(relaying))
            )
            plan[chunks - 1].append(lambda w=w: late_sweep(w, 0, n, relaying))
            plan[chunks - 1].append(
                lambda w=w: late_sweep(w, split, n - split, jnp.logical_not(relaying))
            )
        else:
            plan[chunks - 1].append(lambda w=w: late_sweep(w, 0, n, z >= 0))
    far_at = (chunks * 2 + 2) // 3 - 1
    far_pieces = [list(range(2 * k, min(2 * k + 2, chunks))) for k in range(chunks)]
    if chunks == 1:
        far_pieces = [[0]]
    for k in range(chunks):
        for w in late:
            pass_on(w, k)
        for j in far_pieces[k]:
            for i in lay.far:
                plane_wait(i, j)
                if C > 1:
                    sibling_copy(i, j).start()
        if C > 1 and k == 0:
            for i in lay.near:
                for j in range(chunks):
                    sibling_wait(i, j)
        if k == far_at:
            for i in lay.far:
                order_wait(i)
                if C > 1:
                    order_across(i, 0).start()
            if C > 1:
                for i in lay.far:
                    order_across(i, 1).wait_recv()
        if C > 1 and k == far_at:
            for i in lay.far:
                for j in range(chunks):
                    sibling_wait(i, j)
        for run in plan[k]:
            run()

    for w in late:
        give_back(w)

    for one in range(lay.chips):
        flat = jnp.max(col_best[one], axis=0, keepdims=True)
        for core_at in range(C):
            plane_res[one * C + core_at] = flat[:, core_at * n:(core_at + 1) * n]

    def result_copy(o):
        df, dx, dc = lay.peers[o]
        there = (lax.rem(f + df, F) * X + lax.rem(x + dx, X)) * C + lax.rem(core + dc, C)
        return remote(
            plane_res.at[there], plane_in.at[o], rs.at[o], rr.at[o], plane_id(df, dx, dc)
        )

    for o in range(len(lay.peers)):
        result_copy(o).start()

    best = jnp.maximum(plane_res[slot], jnp.float32(-1.0))
    for o in range(len(lay.peers)):
        result_copy(o).wait_recv()
        best = jnp.maximum(best, plane_in[o])
    line_best[...] = best.reshape(1, n)
    for src in range(S):
        def gather(src=src):
            remote(
                line_res.at[0], line_in.at[src], lrs.at[0], lrr.at[src], line_id(z)
            ).wait_recv()
            line_best[...] = jnp.maximum(line_best[...], line_in[src])

        pl.when(meets(z, jnp.int32(src)))(gather)

    out[...] = line_best[...].reshape(n)
    for k in range(chunks):
        pl.when(sends_up)(lambda k=k: line_copy(own_part(k), k, 1, lay.top + 1, z + 1).wait_send())
        if lay.down:
            pl.when(sends_down)(lambda k=k: line_copy(own_part(k), k, 0, 0, z - 1).wait_send())
        for i in lay.near:
            plane_copy(i, k).wait_send()
        for i in lay.far:
            relay_copy(i, k).wait_send()
        if C > 1:
            for i in range(-1, len(lay.offsets)):
                sibling_copy(i, k).wait_send()
        for w in range(1, lay.top + 1):
            for cond, copy in relays(w, k):
                pl.when(cond)(lambda copy=copy: copy.wait_send())
    for o in range(len(lay.peers)):
        result_copy(o).wait_send()
    for i in lay.near:
        order_copy(i).wait_send()
    for i in lay.far:
        order_relay(i).wait_send()
    if C > 1:
        for i in range(-1, len(lay.offsets)):
            order_across(i, 0).wait_send()
    pl.when(sends_up)(lambda: own_order(z + 1).wait_send())
    if lay.down:
        pl.when(sends_down)(lambda: own_order(z - 1).wait_send())
    for w in range(1, lay.top + 1):
        pl.when(goes_on(w))(lambda w=w: order_up(w).wait_send())
    for w in range(lay.top + 1):
        if w == 0 and not lay.down:
            continue
        pl.when(valid(w))(lambda w=w: line_result(w).wait_send())


def shards(lay, embeddings, doc_order):
    n, depth = embeddings.shape
    chunks = n // PIECE if n % PIECE == 0 else 1
    dma = pltpu.SemaphoreType.DMA
    near, peers, top, S = max(len(lay.offsets), 1), max(len(lay.peers), 1), lay.top, lay.slow
    found = pl.pallas_call(
        functools.partial(kernel, lay, n, chunks),
        out_shape=jax.ShapeDtypeStruct((n,), jnp.float32),
        in_specs=[pl.BlockSpec(memory_space=pltpu.VMEM)] * 2,
        out_specs=pl.BlockSpec(memory_space=pltpu.VMEM),
        scratch_shapes=[
            pltpu.VMEM((lay.plane * n, depth), jnp.bfloat16),
            pltpu.VMEM((top + 1, n, depth), jnp.bfloat16),
            pltpu.VMEM((lay.plane, 1, n), jnp.int32),
            pltpu.VMEM((S, 1, n), jnp.int32),
            pltpu.VMEM((top + 2, n, LANES), jnp.int32),
            pltpu.VMEM((top + 1, n, LANES), jnp.float32),
            pltpu.VMEM((lay.chips, 8, lay.cores * n), jnp.float32),
            pltpu.VMEM((lay.plane, 1, n), jnp.float32),
            pltpu.VMEM((top + 1, 1, n), jnp.float32),
            pltpu.VMEM((peers, 1, n), jnp.float32),
            pltpu.VMEM((S, 1, n), jnp.float32),
            pltpu.VMEM((1, n), jnp.float32),
            dma((near, chunks)), dma((near, chunks)),
            dma((near + 1, chunks)), dma((near + 1, chunks)),
            dma((top + 2, chunks)), dma((top + 1, chunks)),
            dma((near,)), dma((near,)),
            dma((top + 1,)), dma((S,)),
            dma((near + 1,)), dma((near + 1,)),
            dma((peers,)), dma((peers,)),
            dma((top + 1,)), dma((S,)),
        ],
        compiler_params=pltpu.CompilerParams(
            collective_id=0, has_side_effects=True, vmem_limit_bytes=60 * 1024 * 1024
        ),
    )(embeddings, doc_order)
    return found


def solution(mesh):
    lay = Layout(mesh.shape["row"], mesh.shape["col"])
    return jax.shard_map(
        functools.partial(shards, lay),
        mesh=mesh,
        in_specs=(P(("row", "col"), None), P(("row", "col"))),
        out_specs=P(("row", "col")),
        check_vma=False,
    )
```

profile of v0, /device:TPU:0, one launch (start us, length us, event | category | flops | bytes accessed | tf_op | source)
XLA Modules:
  0.0 45.9 jit_solution(8619153619026612643)
XLA Ops:
  0.0 44.6 %shard_map.28 = f32[384]{0:T(512)} custom-call(bf16[384,768]{1,0:T(8,128)(2,1)} %emb.1, s32[384]{0:T(512)} %order.1), custom_call_target="tpu_custom_call" | custom-call | tf_op jit(solution)/shard_map/pallas_call | solution.py:491
  44.6 1.3 %copy.4 = f32[384]{0:T(512)} copy(f32[384]{0:T(512)} %shard_map.28) | data formatting | bytes 3072
where the time goes:
time: 46.1 us; the launch traced here: 45.9 us
  Pallas kernels  44.6 us (97%)
  local copies, waits for them, and re-layouts  1.26 us (3%)
    pallas_call x1, Pallas kernels, shards(): pl.pallas_call(functools.partial(kernel, lay, n, chunks), out_shape=jax.S...  44.6 us
    unnamed x1, local copies, waits for them, and re-layouts  1.26 us

commit v1 on v0

v1 whole, which is shorter than its diff:
```python
import functools

import jax
import jax.numpy as jnp
from jax import lax
from jax.experimental import pallas as pl
from jax.experimental.pallas import tpu as pltpu
from jax.sharding import PartitionSpec as P

MESH = pl.DeviceIdType.MESH
LANES = 128
PIECE = 64


def fast_size(rows):
    best = 1
    for size in range(1, rows + 1):
        if rows % size == 0 and size * size <= rows:
            best = size
    return best


class Layout:
    def __init__(self, rows, cols):
        self.fast = fast_size(rows)
        self.slow = rows // self.fast
        self.cores = 2 if cols % 2 == 0 else 1
        self.xs = cols // self.cores
        self.chips = self.fast * self.xs
        self.plane = self.chips * self.cores
        self.down = self.slow > 2
        self.slots = max(self.slow - 2, 1) + 1
        chips = [(f, x) for f in range(self.fast) for x in range(self.xs)]
        near = [c for c in chips if (c[0] == 0) != (c[1] == 0)]
        far = [c for c in chips if c[0] != 0 and c[1] != 0]
        self.offsets = near + far
        self.near = list(range(len(near)))
        self.far = list(range(len(near), len(near) + len(far)))


def kernel(
    lay, n, chunks,
    emb, order, out,
    raw, own_order, units, line, orders, line_orders, col_orders,
    row_best, col_best, plane_res, line_res, plane_in, line_in,
    load, ps, pr, fr, sr, ls, lr, os_, or_, osr, los, lor, rs, rr, lrs, lrr,
):
    S, F, X, C = lay.slow, lay.fast, lay.xs, lay.cores
    own = lay.slots
    last = S - 1
    rows_here = n // chunks
    align = PIECE if rows_here % PIECE == 0 else rows_here
    r, c = lax.axis_index("row"), lax.axis_index("col")
    z, f = r // F, lax.rem(r, F)
    x, core = c // C, lax.rem(c, C)
    chip = f * X + x
    slot = chip * C + core

    def plane_id(df, dx, dc):
        return {
            "row": z * F + lax.rem(f + df, F),
            "col": lax.rem(x + dx, X) * C + lax.rem(core + dc, C),
        }

    def line_id(there):
        return {"row": there * F + f, "col": c}

    def source_chip(df, dx):
        return lax.rem(f + F - df, F) * X + lax.rem(x + X - dx, X)

    def span(which, k, count=1):
        return pl.ds(pl.multiple_of(which * n + k * rows_here, align), count * rows_here)

    def remote(src, dst, send, recv, where):
        return pltpu.make_async_remote_copy(
            src_ref=src, dst_ref=dst, send_sem=send, recv_sem=recv,
            device_id=where, device_id_type=MESH,
        )

    def here(part, sem):
        return remote(part, part, sem, sem, plane_id(0, 0, 1))

    pairs = [(k, min(2, chunks - k)) for k in range(0, chunks, 2)]

    def plane_copy(i, k):
        part = units.at[span(slot, k)]
        return remote(part, part, ps, pr.at[i, k], plane_id(*lay.offsets[i], 0))

    def relay_copy(i, k):
        df, dx = lay.offsets[i]
        src, step = ((0, dx), (df, 0)) if k % 2 == 0 else ((df, 0), (0, dx))
        part = units.at[span(source_chip(*src) * C + core, k)]
        return remote(part, part, ps, fr.at[i - len(lay.near), k // 2], plane_id(*step, 0))

    def sibling_copy(i, k, count):
        src = chip if i < 0 else source_chip(*lay.offsets[i])
        part = units.at[span(src * C + core, k, count)]
        return remote(part, part, ps, sr.at[i + 1], plane_id(0, 0, 1))

    def near_wait(i, k):
        src = source_chip(*lay.offsets[i]) * C + core
        here(units.at[span(src, k)], pr.at[i, k]).wait_recv()

    def far_wait(i, g):
        src = source_chip(*lay.offsets[i]) * C + core
        k, count = pairs[g]
        here(units.at[span(src, k, count)], fr.at[i - len(lay.near), g]).wait_recv()

    def sibling_wait(i):
        src = chip if i < 0 else source_chip(*lay.offsets[i])
        part = units.at[span(src * C + lax.rem(core + 1, C), 0, chunks)]
        here(part, sr.at[i + 1]).wait_recv()

    sends_up = z < last
    relays_up = (z > 0) & (z < S - 2)
    sends_down = z == last
    transit = z < last
    relays_down = (z > 0) & (z < last)

    def meets(src, dst):
        found = ((src < dst) & (dst < last)) | ((src == last - 1) & (dst == last))
        if lay.down:
            found = found | ((src == last) & (dst < last - 1))
        return found

    def source(w):
        return last if w == 0 else z - w

    def valid(w):
        if w == 0:
            return z < last - 1
        found = (z >= w) & (z < last)
        return (found | (z == last)) if w == 1 else found

    def line_copy(src, k, dst_slot, tag, there):
        return remote(
            src, line.at[dst_slot, pl.ds(k * rows_here, rows_here)],
            ls.at[tag], lr.at[dst_slot, k], line_id(there),
        )

    def own_part(k):
        return units.at[span(slot, k)]

    def slot_part(w, k):
        return line.at[w, pl.ds(k * rows_here, rows_here)]

    def own_up(k):
        return line_copy(own_part(k), k, 1, 0, z + 1)

    def own_down(k):
        return line_copy(own_part(k), k, 0, 0, z - 1)

    def relay_up(w, k):
        return line_copy(slot_part(w, k), k, w + 1, 1 + w, z + 1)

    def relay_down(k):
        return line_copy(slot_part(0, k), k, 0, 1, z - 1)

    def line_wait(w, k):
        here(slot_part(w, k), lr.at[w, k]).wait_recv()

    def line_order(src, dst_slot, tag, there):
        return remote(src, line_orders.at[dst_slot], los.at[tag], lor.at[dst_slot], line_id(there))

    def order_up():
        return line_order(orders.at[slot], 1, 0, z + 1)

    def order_down():
        return line_order(orders.at[slot], 0, 0, z - 1)

    def order_on_up(w):
        return line_order(line_orders.at[w], w + 1, 1 + w, z + 1)

    def order_on_down():
        return line_order(line_orders.at[0], 0, 1, z - 1)

    def order_send(src, sem, where):
        return remote(orders.at[src], orders.at[src], os_, sem, where)

    def order_copy(i):
        return order_send(slot, or_.at[i], plane_id(*lay.offsets[i], 0))

    def order_relay(i):
        df, dx = lay.offsets[i]
        return order_send(source_chip(0, dx) * C + core, or_.at[i], plane_id(df, 0, 0))

    def order_wait(i):
        src = source_chip(*lay.offsets[i]) * C + core
        here(orders.at[src], or_.at[i]).wait_recv()

    def order_across(i):
        src = chip if i < 0 else source_chip(*lay.offsets[i])
        return order_send(src * C + core, osr.at[i + 1], plane_id(0, 0, 1))

    def order_across_wait(i):
        src = chip if i < 0 else source_chip(*lay.offsets[i])
        here(orders.at[src * C + lax.rem(core + 1, C)], osr.at[i + 1]).wait_recv()

    barrier = pltpu.get_barrier_semaphore()
    steps = [(*lay.offsets[i], 0) for i in lay.near] + ([(0, 0, 1)] if C > 1 else [])
    sides = ((z > 0, z - 1), (z < last, z + 1))
    for step in steps:
        pl.semaphore_signal(barrier, inc=1, device_id=plane_id(*step), device_id_type=MESH)
    for there, which in sides:
        pl.when(there)(
            lambda which=which: pl.semaphore_signal(
                barrier, inc=1, device_id=line_id(which), device_id_type=MESH
            )
        )
    loads = [
        pltpu.make_async_copy(emb, raw, load.at[0]),
        pltpu.make_async_copy(order, own_order, load.at[1]),
    ]
    for one in loads:
        one.start()
    row_best[...] = jnp.full(row_best.shape, -1.0, jnp.float32)
    col_best[...] = jnp.full(col_best.shape, -1.0, jnp.float32)
    loads[1].wait()
    orders[pl.ds(slot, 1)] = own_order[...].reshape(1, 1, n)
    loads[0].wait()

    def normalize(k):
        floats = raw[pl.ds(k * rows_here, rows_here), :].astype(jnp.float32)
        scale = lax.rsqrt(jnp.sum(floats * floats, axis=1, keepdims=True) + 1e-06)
        units[span(slot, k), :] = (floats * scale).astype(jnp.bfloat16)

    for k in range(chunks):
        normalize(k)
    lines = jnp.minimum(z, 1) + jnp.minimum(last - z, 1)
    pl.semaphore_wait(barrier, len(steps) + lines)

    def start(cond, *copies):
        @pl.when(cond)
        def run():
            for one in copies:
                one().start()

    early = (chunks + 1) // 2
    if S > 1:
        start(sends_up, order_up, *[functools.partial(own_up, k) for k in range(early)])
        start(sends_up & jnp.logical_not(relays_up),
              *[functools.partial(own_up, k) for k in range(early, chunks)])
    if lay.down:
        start(sends_down, order_down, *[functools.partial(own_down, k) for k in range(chunks)])
    for i in lay.near:
        order_copy(i).start()
    if C > 1:
        order_across(-1).start()
        sibling_copy(-1, 0, chunks).start()
    for k in range(chunks):
        for i in lay.near:
            plane_copy(i, k).start()

    def spread(which, row):
        wide = jnp.broadcast_to(row.reshape(1, n), (LANES, n))
        col_orders[which] = wide.T

    spread(own, orders[slot])

    width = C * n

    def item(lhs, w, first_chip, both, first=0, count=n, wide=1):
        rhs = units[pl.ds(pl.multiple_of(first_chip * width, LANES), wide * width), :]
        s = lax.dot_general(
            lhs, rhs, (((1,), (1,)), ((), ())), preferred_element_type=jnp.float32
        )
        mine = col_orders[w, first:first + count, :]
        rows_max = None
        for j in range(wide * width // LANES):
            part = s[:, j * LANES:(j + 1) * LANES]
            which_chip, at = first_chip + j * LANES // width, j * LANES % width
            core_at, lane_at = at // n, at % n
            theirs = orders[which_chip * C + core_at, :, lane_at:lane_at + LANES]
            earlier = theirs < mine
            if both:
                cand = jnp.where(earlier, part, jnp.float32(-1.0))
                rows_max = cand if rows_max is None else jnp.maximum(rows_max, cand)
                later = jnp.where(earlier, jnp.float32(-1.0), part)
            else:
                later = jnp.where(mine < theirs, part, jnp.float32(-1.0))
            down = jnp.max(later.reshape(count // 8, 8, LANES), axis=0)
            col_best[which_chip, :, at:at + LANES] = jnp.maximum(
                col_best[which_chip, :, at:at + LANES], down
            )
        if both:
            row_best[w, first:first + count, :] = jnp.maximum(
                row_best[w, first:first + count, :], rows_max
            )

    def own_item(which_chip):
        lhs = units[pl.ds(pl.multiple_of(slot * n, LANES), n), :]
        item(lhs, own, which_chip, False)

    def chips_of(places):
        def at(j):
            if places == "near":
                by_x = j < X - 1
                df = jnp.where(by_x, 0, j - (X - 2))
                dx = jnp.where(by_x, j + 1, 0)
            elif places == "far":
                df, dx = 1 + j // max(X - 1, 1), 1 + lax.rem(j, max(X - 1, 1))
            else:
                df, dx = 0, 0
            return source_chip(df, dx)

        return {"near": F + X - 2, "far": (F - 1) * (X - 1), "self": 1}[places], at

    def loop(places, body):
        count, at = chips_of(places)

        def step(j, carry):
            body(at(j))
            return carry

        if count == 1:
            body(at(0))
        elif count:
            lax.fori_loop(0, count, step, 0)

    def line_sweep(w, places, first, count, cond):
        @pl.when(valid(w) & cond)
        def run():
            loop(places, lambda one: item(
                line[w, first:first + count, :], w, one, True, first, count
            ))

    wide = next(m for m in (4, 3, 2, 1) if lay.chips % m == 0)

    def wide_sweep(w, first, count, cond):
        def body(j, carry):
            item(line[w, first:first + count, :], w, j * wide, True, first, count, wide)
            return carry

        @pl.when(valid(w) & cond)
        def run():
            lax.fori_loop(0, lay.chips // wide, body, 0)

    for i in lay.near:
        order_wait(i)
        if C > 1:
            order_across(i).start()
    for i in lay.far:
        order_relay(i).start()

    def take_order(w):
        if w == 0 and not lay.down:
            return
        arrives = transit if w == 0 else valid(w)

        @pl.when(arrives)
        def run():
            here(line_orders.at[w], lor.at[w]).wait_recv()
            if w == 0:
                pl.when(relays_down)(lambda: order_on_down().start())
            elif w < S - 2:
                pl.when(relays_up)(lambda: order_on_up(w).start())

        pl.when(valid(w))(lambda: spread(w, line_orders[w]))

    if S > 1:
        take_order(1)
    if C > 1:
        order_across_wait(-1)
        sibling_wait(-1)
    own_item(chip)
    if C > 1:
        for i in lay.near:
            order_across_wait(i)

    held = (z > 1) & (z < last) if S > 3 else z < 0
    straight = jnp.logical_not(held)
    half = early * rows_here

    def take_first(k):
        cond = valid(1) if k < early else valid(1) & straight

        @pl.when(cond)
        def run():
            line_wait(1, k)
            if S > 3:
                pl.when(relays_up)(lambda: relay_up(1, k).start())

    def take_last(k):
        @pl.when(valid(1) & held)
        def run():
            line_wait(1, k)
            if S > 4:
                pl.when(relays_up)(lambda: relay_up(1, k).start())

    def take_down(p):
        if not lay.down:
            return
        for there in range(S - 2, 0, -1):
            k = p - 2 * (S - 2 - there)
            if 0 <= k < chunks:
                @pl.when(z == there)
                def run(k=k):
                    line_wait(0, k)
                    relay_down(k).start()

    for k in range(chunks):
        if S > 1:
            take_first(k)
        for i in lay.near:
            near_wait(i, k)
        for i in lay.far:
            relay_copy(i, k).start()
        if C > 1:
            for i in lay.near:
                sibling_copy(i, k, 1).start()
        if k == 0:
            take_order(0)
        take_down(k)
    if S > 3:
        start(relays_up, *[functools.partial(own_up, k) for k in range(early, chunks)])

    def far_group(g):
        for i in lay.far:
            far_wait(i, g)
            if C > 1:
                sibling_copy(i, *pairs[g]).start()

    always = z >= 0
    if C > 1:
        for i in lay.near:
            sibling_wait(i)
    loop("near", own_item)
    more = list(range(chunks, chunks + 2 * max(S - 3, 0)))
    for p in more[:1]:
        take_down(p)
    for i in lay.far:
        order_wait(i)
        if C > 1:
            order_across(i).start()
    far_group(0)
    if S > 1:
        line_sweep(1, "self", 0, n, straight)
        if S > 3:
            line_sweep(1, "self", 0, half, held)
    for p in more[1:]:
        take_down(p)
    if S > 1:
        line_sweep(1, "near", 0, n, straight)
        if S > 3:
            line_sweep(1, "near", 0, half, held)
    for g in range(1, len(pairs)):
        far_group(g)

    if lay.down:
        @pl.when(z == 0)
        def run():
            for k in range(chunks):
                line_wait(0, k)
        line_sweep(0, "self", 0, n, always)
        line_sweep(0, "near", 0, n, always)
    for w in range(2, S - 1):
        @pl.when(valid(w))
        def run(w=w):
            for k in range(chunks):
                line_wait(w, k)
                if w < S - 2:
                    pl.when(z < S - 2)(lambda: relay_up(w, k).start())
            here(line_orders.at[w], lor.at[w]).wait_recv()
            if w < S - 2:
                pl.when(z < S - 2)(lambda: order_on_up(w).start())
            spread(w, line_orders[w])
        line_sweep(w, "self", 0, n, always)
        line_sweep(w, "near", 0, n, always)

    if C > 1:
        for i in lay.far:
            order_across_wait(i)
            sibling_wait(i)
    loop("far", own_item)
    order_of_slots = ([0] if lay.down else []) + list(range(2, S - 1))
    for w in order_of_slots:
        line_sweep(w, "far", 0, n, always)
    if S > 1:
        line_sweep(1, "far", 0, n, straight)
        if S > 3:
            line_sweep(1, "far", 0, half, held)

    def line_result(w):
        return remote(line_res.at[w], line_in.at[z], lrs.at[w], lrr.at[z], line_id(source(w)))

    def give_back(w, cond):
        @pl.when(valid(w) & cond)
        def fold():
            line_res[w] = jnp.max(row_best[w].T, axis=0, keepdims=True)
            line_result(w).start()

    for w in order_of_slots:
        give_back(w, always)
    if S > 1:
        give_back(1, straight)
    if S > 3:
        for k in range(early, chunks - 1):
            take_last(k)
        if chunks - 1 > early:
            wide_sweep(1, half, (chunks - 1 - early) * rows_here, held)
        if chunks > early:
            take_last(chunks - 1)
            wide_sweep(1, (chunks - 1) * rows_here, rows_here, held)
        give_back(1, held)

    def result_copy(df, dx, dc):
        there = (lax.rem(f + df, F) * X + lax.rem(x + dx, X)) * C + lax.rem(core + dc, C)
        o = (df * X + dx) * C + dc
        return remote(plane_res.at[there], plane_in.at[o], rs, rr, plane_id(df, dx, dc))

    def flush(df, dx):
        one = lax.rem(f + df, F) * X + lax.rem(x + dx, X)
        flat = jnp.max(col_best[one], axis=0, keepdims=True)
        for core_at in range(C):
            plane_res[one * C + core_at] = flat[:, core_at * n:(core_at + 1) * n]

    def flush_out(j, carry):
        df, dx = (lay.chips - 1 - j) // X, lax.rem(lay.chips - 1 - j, X)
        flush(df, dx)
        for dc in range(C):
            result_copy(df, dx, dc).start()
        return carry

    lax.fori_loop(0, lay.chips - 1, flush_out, 0)
    flush(0, 0)
    if C > 1:
        result_copy(0, 0, 1).start()

    best = jnp.maximum(plane_res[slot], jnp.float32(-1.0))
    if lay.plane > 1:
        here(plane_in.at[pl.ds(1, lay.plane - 1)], rr).wait_recv()
        best = jnp.maximum(best, jnp.max(plane_in[1:], axis=0))
    plane_res[slot] = best
    for src in range(S):
        def gather(src=src):
            here(line_in.at[src], lrr.at[src]).wait_recv()
            plane_res[slot] = jnp.maximum(plane_res[slot], line_in[src])

        pl.when(meets(z, jnp.int32(src)))(gather)
    out[...] = plane_res[slot].reshape(n)

    def sent(part, sem):
        here(part, sem).wait_send()

    if lay.plane > 1:
        sent(units.at[pl.ds(0, (lay.plane - 1) * n)], ps)
        sent(orders.at[pl.ds(0, lay.plane - 1)], os_)
        sent(plane_in.at[pl.ds(1, lay.plane - 1)], rs)

    def line_sent(cond, tag):
        @pl.when(cond)
        def run():
            sent(line.at[0], ls.at[tag])
            sent(line_orders.at[0], los.at[tag])

    if S > 1:
        line_sent((sends_up | sends_down) if lay.down else sends_up, 0)
    if lay.down:
        line_sent(relays_down, 1)
    for w in range(1, S - 2):
        line_sent(valid(w) & (z < S - 2), 1 + w)
    for w in range(lay.slots):
        if S > 1 and (w or lay.down):
            pl.when(valid(w))(lambda w=w: sent(line_res.at[w], lrs.at[w]))


def shards(lay, embeddings, doc_order):
    n, depth = embeddings.shape
    chunks = n // PIECE if n % PIECE == 0 else 1
    dma = pltpu.SemaphoreType.DMA
    S, near, far = lay.slow, max(len(lay.near), 1), max(len(lay.far), 1)
    vmem = pltpu.VMEM
    return pl.pallas_call(
        functools.partial(kernel, lay, n, chunks),
        out_shape=vmem((n,), jnp.float32),
        in_specs=[pl.BlockSpec(memory_space=pl.ANY)] * 2,
        out_specs=pl.BlockSpec(memory_space=vmem),
        scratch_shapes=[
            vmem((n, depth), jnp.bfloat16),
            vmem((n,), jnp.int32),
            vmem((lay.plane * n, depth), jnp.bfloat16),
            vmem((lay.slots, n, depth), jnp.bfloat16),
            vmem((lay.plane, 1, n), jnp.int32),
            vmem((lay.slots, 1, n), jnp.int32),
            vmem((lay.slots + 1, n, LANES), jnp.int32),
            vmem((lay.slots, n, LANES), jnp.float32),
            vmem((lay.chips, 8, lay.cores * n), jnp.float32),
            vmem((lay.plane, 1, n), jnp.float32),
            vmem((lay.slots, 1, n), jnp.float32),
            vmem((lay.plane, 1, n), jnp.float32),
            vmem((S, 1, n), jnp.float32),
            dma((2,)),
            dma(()), dma((near, chunks)), dma((far, (chunks + 1) // 2)), dma((near + far + 1,)),
            dma((S,)), dma((lay.slots, chunks)),
            dma(()), dma((near + far,)), dma((near + far + 1,)),
            dma((S,)), dma((lay.slots,)),
            dma(()), dma(()),
            dma((lay.slots,)), dma((S,)),
        ],
        compiler_params=pltpu.CompilerParams(
            collective_id=0, has_side_effects=True, vmem_limit_bytes=60 * 1024 * 1024
        ),
    )(embeddings, doc_order)


def solution(mesh):
    lay = Layout(mesh.shape["row"], mesh.shape["col"])
    return jax.shard_map(
        functools.partial(shards, lay),
        mesh=mesh,
        in_specs=(P(("row", "col"), None), P(("row", "col"))),
        out_specs=P(("row", "col")),
        check_vma=False,
    )
```

time: 46.1 us -> 36.7 us (0.80)
  Pallas kernels: 44.6 us -> 36 us
  local copies, waits for them, and re-layouts: 1.26 us -> 0.58 us
    pallas_call x1, Pallas kernels: 44.6 us -> 36 us  [shards(): pl.pallas_call(functools.partial(kernel, lay, n, chunks), out_shape=vmem(...]
    unnamed x1, local copies, waits for them, and re-layouts: 1.26 us -> 0.58 us
where the time goes in v1:
time: 36.7 us; the launch traced here: 36.6 us
  Pallas kernels  36 us (98%)
  local copies, waits for them, and re-layouts  0.58 us (2%)
    pallas_call x1, Pallas kernels, shards(): pl.pallas_call(functools.partial(kernel, lay, n, chunks), out_shape=vmem(...  36 us

profile of v1, /device:TPU:0, one launch (start us, length us, event | category | flops | bytes accessed | tf_op | source)
XLA Modules:
  0.0 36.6 jit_solution(9507231233277269413)
XLA Ops:
  0.0 36.0 %shard_map.28 = f32[384]{0:T(512)S(1)} custom-call(bf16[384,768]{1,0:T(8,128)(2,1)} %emb.1, s32[384]{0:T(512)} %order.1), custom_call_target="tpu_custom_call" | custom-call | tf_op jit(solution)/shard_map/pallas_call | solution.py:573
  36.0 0.6 %copy.4 = f32[384]{0:T(512)} copy(f32[384]{0:T(512)S(1)} %shard_map.28) | data formatting | bytes 3072

commit v2 on v1

--- a/solution.py
+++ b/solution.py
@@ -30,6 +30,7 @@
         self.plane = self.chips * self.cores
         self.down = self.slow > 2
         self.slots = max(self.slow - 2, 1) + 1
+        self.hold = self.slow == 4
         chips = [(f, x) for f in range(self.fast) for x in range(self.xs)]
         near = [c for c in chips if (c[0] == 0) != (c[1] == 0)]
         far = [c for c in chips if c[0] != 0 and c[1] != 0]
@@ -112,16 +113,12 @@
         here(part, sr.at[i + 1]).wait_recv()
 
     sends_up = z < last
-    relays_up = (z > 0) & (z < S - 2)
     sends_down = z == last
-    transit = z < last
-    relays_down = (z > 0) & (z < last)
+    relays_down = (z > 0) & (z < last - 1)
 
     def meets(src, dst):
         found = ((src < dst) & (dst < last)) | ((src == last - 1) & (dst == last))
-        if lay.down:
-            found = found | ((src == last) & (dst < last - 1))
-        return found
+        return found | ((src == last) & (dst < last - 1)) if lay.down else found
 
     def source(w):
         return last if w == 0 else z - w
@@ -132,6 +129,9 @@
         found = (z >= w) & (z < last)
         return (found | (z == last)) if w == 1 else found
 
+    def goes_on(w):
+        return (z >= w) & (z < last - 1)
+
     def line_copy(src, k, dst_slot, tag, there):
         return remote(
             src, line.at[dst_slot, pl.ds(k * rows_here, rows_here)],
@@ -148,7 +148,7 @@
         return line_copy(own_part(k), k, 1, 0, z + 1)
 
     def own_down(k):
-        return line_copy(own_part(k), k, 0, 0, z - 1)
+        return line_copy(own_part(k), k, 0, 0, z - 2)
 
     def relay_up(w, k):
         return line_copy(slot_part(w, k), k, w + 1, 1 + w, z + 1)
@@ -166,7 +166,7 @@
         return line_order(orders.at[slot], 1, 0, z + 1)
 
     def order_down():
-        return line_order(orders.at[slot], 0, 0, z - 1)
+        return line_order(orders.at[slot], 0, 0, z - 2)
 
     def order_on_up(w):
         return line_order(line_orders.at[w], w + 1, 1 + w, z + 1)
@@ -198,7 +198,7 @@
 
     barrier = pltpu.get_barrier_semaphore()
     steps = [(*lay.offsets[i], 0) for i in lay.near] + ([(0, 0, 1)] if C > 1 else [])
-    sides = ((z > 0, z - 1), (z < last, z + 1))
+    sides = ((z > 0, z - 1), (z < last, z + 1), (z == last - 2, z + 2))
     for step in steps:
         pl.semaphore_signal(barrier, inc=1, device_id=plane_id(*step), device_id_type=MESH)
     for there, which in sides:
@@ -227,6 +227,8 @@
     for k in range(chunks):
         normalize(k)
     lines = jnp.minimum(z, 1) + jnp.minimum(last - z, 1)
+    if lay.down:
+        lines = lines + z // last
     pl.semaphore_wait(barrier, len(steps) + lines)
 
     def start(cond, *copies):
@@ -235,10 +237,11 @@
             for one in copies:
                 one().start()
 
-    early = (chunks + 1) // 2
+    early = (chunks + 2) // 3 if lay.hold else chunks
+    holds = z == 1 if lay.hold else z < 0
     if S > 1:
         start(sends_up, order_up, *[functools.partial(own_up, k) for k in range(early)])
-        start(sends_up & jnp.logical_not(relays_up),
+        start(sends_up & jnp.logical_not(holds),
               *[functools.partial(own_up, k) for k in range(early, chunks)])
     if lay.down:
         start(sends_down, order_down, *[functools.partial(own_down, k) for k in range(chunks)])
@@ -246,10 +249,11 @@
         order_copy(i).start()
     if C > 1:
         order_across(-1).start()
-        sibling_copy(-1, 0, chunks).start()
     for k in range(chunks):
         for i in lay.near:
             plane_copy(i, k).start()
+        if C > 1 and k == 0:
+            sibling_copy(-1, 0, chunks).start()
 
     def spread(which, row):
         wide = jnp.broadcast_to(row.reshape(1, n), (LANES, n))
@@ -259,11 +263,13 @@
 
     width = C * n
 
-    def item(lhs, w, first_chip, both, first=0, count=n, wide=1):
+    def scores(lhs, first_chip, wide=1):
         rhs = units[pl.ds(pl.multiple_of(first_chip * width, LANES), wide * width), :]
-        s = lax.dot_general(
+        return lax.dot_general(
             lhs, rhs, (((1,), (1,)), ((), ())), preferred_element_type=jnp.float32
         )
+
+    def fold(s, w, first_chip, both, first=0, count=n, wide=1):
         mine = col_orders[w, first:first + count, :]
         rows_max = None
         for j in range(wide * width // LANES):
@@ -287,9 +293,22 @@
                 row_best[w, first:first + count, :], rows_max
             )
 
+    def own_rows():
+        return units[pl.ds(pl.multiple_of(slot * n, LANES), n), :]
+
     def own_item(which_chip):
-        lhs = units[pl.ds(pl.multiple_of(slot * n, LANES), n), :]
-        item(lhs, own, which_chip, False)
+        fold(scores(own_rows(), which_chip), own, which_chip, False)
+
+    def run_all(jobs):
+        ready = None
+        for w, first, count, one in jobs:
+            lhs = own_rows() if w == own else line[w, first:first + count, :]
+            s = scores(lhs, one)
+            if ready is not None:
+                fold(*ready)
+            ready = (s, w, one, w != own, first, count)
+        if ready is not None:
+            fold(*ready)
 
     def chips_of(places):
         def at(j):
@@ -305,30 +324,30 @@
 
         return {"near": F + X - 2, "far": (F - 1) * (X - 1), "self": 1}[places], at
 
-    def loop(places, body):
+    def sweep(places, rows):
         count, at = chips_of(places)
 
         def step(j, carry):
-            body(at(j))
+            run_all([(*one, at(j)) for one in rows])
             return carry
 
-        if count == 1:
-            body(at(0))
-        elif count:
+        if count <= 2:
+            run_all([(*one, at(j)) for j in range(count) for one in rows])
+        else:
             lax.fori_loop(0, count, step, 0)
 
     def line_sweep(w, places, first, count, cond):
-        @pl.when(valid(w) & cond)
-        def run():
-            loop(places, lambda one: item(
-                line[w, first:first + count, :], w, one, True, first, count
-            ))
+        pl.when(valid(w) & cond)(lambda: sweep(places, [(w, first, count)]))
+
+    def sweep_own(places):
+        sweep(places, [(own, 0, n)])
 
     wide = next(m for m in (4, 3, 2, 1) if lay.chips % m == 0)
 
     def wide_sweep(w, first, count, cond):
         def body(j, carry):
-            item(line[w, first:first + count, :], w, j * wide, True, first, count, wide)
+            s = scores(line[w, first:first + count, :], j * wide, wide)
+            fold(s, w, j * wide, True, first, count, wide)
             return carry
 
         @pl.when(valid(w) & cond)
@@ -342,65 +361,51 @@
     for i in lay.far:
         order_relay(i).start()
 
-    def take_order(w):
-        if w == 0 and not lay.down:
-            return
-        arrives = transit if w == 0 else valid(w)
-
-        @pl.when(arrives)
+    def take_order(w, cond):
+        @pl.when(cond)
         def run():
             here(line_orders.at[w], lor.at[w]).wait_recv()
             if w == 0:
                 pl.when(relays_down)(lambda: order_on_down().start())
-            elif w < S - 2:
-                pl.when(relays_up)(lambda: order_on_up(w).start())
-
-        pl.when(valid(w))(lambda: spread(w, line_orders[w]))
+            elif w < last - 1:
+                pl.when(goes_on(w))(lambda: order_on_up(w).start())
+            spread(w, line_orders[w])
 
     if S > 1:
-        take_order(1)
+        take_order(1, valid(1))
     if C > 1:
         order_across_wait(-1)
         sibling_wait(-1)
     own_item(chip)
-    if C > 1:
-        for i in lay.near:
-            order_across_wait(i)
-
-    held = (z > 1) & (z < last) if S > 3 else z < 0
+    held = z == 2 if lay.hold else z < 0
     straight = jnp.logical_not(held)
     half = early * rows_here
 
-    def take_first(k):
-        cond = valid(1) if k < early else valid(1) & straight
-
+    def take(w, k, cond):
         @pl.when(cond)
         def run():
-            line_wait(1, k)
-            if S > 3:
-                pl.when(relays_up)(lambda: relay_up(1, k).start())
-
-    def take_last(k):
-        @pl.when(valid(1) & held)
-        def run():
-            line_wait(1, k)
-            if S > 4:
-                pl.when(relays_up)(lambda: relay_up(1, k).start())
+            line_wait(w, k)
+            if w < last - 1:
+                pl.when(goes_on(w))(lambda: relay_up(w, k).start())
 
     def take_down(p):
-        if not lay.down:
-            return
-        for there in range(S - 2, 0, -1):
-            k = p - 2 * (S - 2 - there)
+        for there in range(S - 3, 0, -1):
+            k = p - 1 - 2 * (S - 3 - there)
+            if k == 0:
+                take_order(0, z == there)
             if 0 <= k < chunks:
                 @pl.when(z == there)
                 def run(k=k):
                     line_wait(0, k)
                     relay_down(k).start()
 
-    for k in range(chunks):
-        if S > 1:
-            take_first(k)
+    def far_group(g):
+        for i in lay.far:
+            far_wait(i, g)
+            if C > 1:
+                sibling_copy(i, *pairs[g]).start()
+
+    def near_chunk(k):
         for i in lay.near:
             near_wait(i, k)
         for i in lay.far:
@@ -408,100 +413,109 @@
         if C > 1:
             for i in lay.near:
                 sibling_copy(i, k, 1).start()
-        if k == 0:
-            take_order(0)
-        take_down(k)
-    if S > 3:
-        start(relays_up, *[functools.partial(own_up, k) for k in range(early, chunks)])
-
-    def far_group(g):
-        for i in lay.far:
-            far_wait(i, g)
-            if C > 1:
-                sibling_copy(i, *pairs[g]).start()
-
-    always = z >= 0
+
+    for p in range(chunks + 2 * max(S - 4, 0) + 1):
+        if p < chunks and S > 1:
+            take(1, p, valid(1) if p < early else valid(1) & straight)
+        for w in range(2, last - 1):
+            k = p - 2 * (w - 1)
+            if k == 0:
+                take_order(w, goes_on(w))
+            if 0 <= k < chunks:
+                take(w, k, goes_on(w))
+        if lay.hold and p == chunks - 1:
+            start(holds, *[functools.partial(own_up, k) for k in range(early, chunks)])
+        take_down(p)
+        if p < chunks:
+            near_chunk(p)
+        if lay.hold and p == early + 1:
+            line_sweep(1, "self", 0, half, held)
     if C > 1:
         for i in lay.near:
+            order_across_wait(i)
             sibling_wait(i)
-    loop("near", own_item)
-    more = list(range(chunks, chunks + 2 * max(S - 3, 0)))
-    for p in more[:1]:
-        take_down(p)
+    sweep_own("near")
     for i in lay.far:
         order_wait(i)
         if C > 1:
             order_across(i).start()
     far_group(0)
+    ends = z == last - 1
+    bottom = z == 0
+
+    def line_result(w):
+        return remote(line_res.at[w], line_in.at[z], lrs.at[w], lrr.at[z], line_id(source(w)))
+
+    def give_back(w, cond):
+        @pl.when(valid(w) & cond)
+        def run():
+            line_res[w] = jnp.max(row_best[w].T, axis=0, keepdims=True)
+            line_result(w).start()
+
+    def take_rows(w, cond):
+        @pl.when(valid(w) & cond)
+        def run():
+            for k in range(chunks):
+                line_wait(w, k)
+        take_order(w, valid(w) & cond)
+
     if S > 1:
         line_sweep(1, "self", 0, n, straight)
-        if S > 3:
-            line_sweep(1, "self", 0, half, held)
-    for p in more[1:]:
-        take_down(p)
+        if lay.hold:
+            line_sweep(1, "near", 0, half, held)
+    if lay.down:
+        line_sweep(0, "self", 0, n, relays_down)
+    for w in range(2, last):
+        take_rows(w, ends)
+        line_sweep(w, "self", 0, n, z < last)
+    for g in range(1, len(pairs) - 1):
+        far_group(g)
     if S > 1:
         line_sweep(1, "near", 0, n, straight)
-        if S > 3:
-            line_sweep(1, "near", 0, half, held)
-    for g in range(1, len(pairs)):
+    for w in range(2, last):
+        line_sweep(w, "near", 0, n, z < last)
+    for g in range(max(len(pairs) - 1, 1), len(pairs)):
         far_group(g)
-
     if lay.down:
-        @pl.when(z == 0)
-        def run():
-            for k in range(chunks):
-                line_wait(0, k)
-        line_sweep(0, "self", 0, n, always)
-        line_sweep(0, "near", 0, n, always)
-    for w in range(2, S - 1):
-        @pl.when(valid(w))
-        def run(w=w):
-            for k in range(chunks):
-                line_wait(w, k)
-                if w < S - 2:
-                    pl.when(z < S - 2)(lambda: relay_up(w, k).start())
-            here(line_orders.at[w], lor.at[w]).wait_recv()
-            if w < S - 2:
-                pl.when(z < S - 2)(lambda: order_on_up(w).start())
-            spread(w, line_orders[w])
-        line_sweep(w, "self", 0, n, always)
-        line_sweep(w, "near", 0, n, always)
-
+        line_sweep(0, "near", 0, n, relays_down)
     if C > 1:
         for i in lay.far:
             order_across_wait(i)
             sibling_wait(i)
-    loop("far", own_item)
-    order_of_slots = ([0] if lay.down else []) + list(range(2, S - 1))
-    for w in order_of_slots:
-        line_sweep(w, "far", 0, n, always)
-    if S > 1:
-        line_sweep(1, "far", 0, n, straight)
-        if S > 3:
-            line_sweep(1, "far", 0, half, held)
-
-    def line_result(w):
-        return remote(line_res.at[w], line_in.at[z], lrs.at[w], lrr.at[z], line_id(source(w)))
-
-    def give_back(w, cond):
-        @pl.when(valid(w) & cond)
-        def fold():
-            line_res[w] = jnp.max(row_best[w].T, axis=0, keepdims=True)
-            line_result(w).start()
-
-    for w in order_of_slots:
-        give_back(w, always)
+    if lay.hold:
+        pl.when(held)(lambda: sweep("far", [(own, 0, n), (2, 0, n), (1, 0, half)]))
+        pl.when(z == 1)(lambda: sweep("far", [(own, 0, n), (0, 0, n), (1, 0, n)]))
+        pl.when(z == last)(lambda: sweep("far", [(own, 0, n), (1, 0, n)]))
+        pl.when(bottom)(lambda: sweep_own("far"))
+    else:
+        sweep_own("far")
+        for w in range(2, last):
+            line_sweep(w, "far", 0, n, z < last)
+        if lay.down:
+            line_sweep(0, "far", 0, n, relays_down)
+        if S > 1:
+            line_sweep(1, "far", 0, n, straight)
+    for w in range(2, last):
+        give_back(w, z < last)
     if S > 1:
         give_back(1, straight)
-    if S > 3:
+    if lay.down:
+        give_back(0, relays_down)
+        take_rows(0, bottom)
+        wide_sweep(0, 0, n, bottom)
+        give_back(0, bottom)
+    final = (chunks - 1) * rows_here
+    tail = final // LANES * LANES
+    if lay.hold:
         for k in range(early, chunks - 1):
-            take_last(k)
+            take(1, k, held)
         if chunks - 1 > early:
-            wide_sweep(1, half, (chunks - 1 - early) * rows_here, held)
-        if chunks > early:
-            take_last(chunks - 1)
-            wide_sweep(1, (chunks - 1) * rows_here, rows_here, held)
-        give_back(1, held)
+            wide_sweep(1, half, final - half, held)
+        if tail:
+            @pl.when(held)
+            def run():
+                line_res[1, :, :tail] = jnp.max(row_best[1, :tail, :].T, axis=0, keepdims=True)
+        take(1, chunks - 1, held)
 
     def result_copy(df, dx, dc):
         there = (lax.rem(f + df, F) * X + lax.rem(x + dx, X)) * C + lax.rem(core + dc, C)
@@ -514,17 +528,47 @@
         for core_at in range(C):
             plane_res[one * C + core_at] = flat[:, core_at * n:(core_at + 1) * n]
 
-    def flush_out(j, carry):
-        df, dx = (lay.chips - 1 - j) // X, lax.rem(lay.chips - 1 - j, X)
+    def flush_out(df, dx, first=0):
         flush(df, dx)
-        for dc in range(C):
+        for dc in range(first, C):
             result_copy(df, dx, dc).start()
-        return carry
-
-    lax.fori_loop(0, lay.chips - 1, flush_out, 0)
-    flush(0, 0)
-    if C > 1:
-        result_copy(0, 0, 1).start()
+
+    def finish():
+        def step(j, carry):
+            flush_out((lay.chips - 1 - j) // X, lax.rem(lay.chips - 1 - j, X))
+            return carry
+
+        if lay.chips > 4:
+            lax.fori_loop(0, lay.chips - 1, step, 0)
+        else:
+            for j in range(lay.chips - 1, 0, -1):
+                flush_out(j // X, j % X)
+        flush_out(0, 0, 1)
+
+    def finish_late():
+        ready = None
+        for j in range(lay.chips - 1, -1, -1):
+            df, dx = j // X, j % X
+            at = lax.rem(f + df, F) * X + lax.rem(x + dx, X)
+            s = scores(line[1, final:, :], at)
+            if ready is not None:
+                fold(*ready[0], 1, ready[1], True, final, n - final)
+                flush_out(*ready[2])
+            ready = (s,), at, (df, dx)
+        fold(*ready[0], 1, ready[1], True, final, n - final)
+        line_res[1, :, tail:] = jnp.max(row_best[1, tail:, :].T, axis=0, keepdims=True)
+        line_result(1).start()
+        flush_out(0, 0, 1)
+
+    if lay.hold and lay.chips <= 4:
+        pl.when(held)(finish_late)
+        pl.when(straight)(finish)
+    elif lay.hold:
+        wide_sweep(1, final, n - final, held)
+        give_back(1, held)
+        finish()
+    else:
+        finish()
 
     best = jnp.maximum(plane_res[slot], jnp.float32(-1.0))
     if lay.plane > 1:
@@ -557,9 +601,9 @@
         line_sent((sends_up | sends_down) if lay.down else sends_up, 0)
     if lay.down:
         line_sent(relays_down, 1)
-    for w in range(1, S - 2):
-        line_sent(valid(w) & (z < S - 2), 1 + w)
-    for w in range(lay.slots):
+    for w in range(1, last - 1):
+        line_sent(goes_on(w), 1 + w)
+    for w in range(S):
         if S > 1 and (w or lay.down):
             pl.when(valid(w))(lambda w=w: sent(line_res.at[w], lrs.at[w]))
 

time: 36.7 us -> 34.9 us (0.951)
  the two profiles are of different devices: /device:TPU:0 before, /device:TPU:17 now
where the time goes in v2:
time: 34.9 us; the launch traced here: 34.7 us
  Pallas kernels  34.1 us (98%)
  local copies, waits for them, and re-layouts  0.58 us (2%)
    pallas_call x1, Pallas kernels, shards(): pl.pallas_call(functools.partial(kernel, lay, n, chunks), out_shape=vmem(...  34.1 us

profile of v2, /device:TPU:17, one launch (start us, length us, event | category | flops | bytes accessed | tf_op | source)
XLA Modules:
  0.0 34.7 jit_solution(13347100290717526937)
XLA Ops:
  0.0 34.1 %shard_map.28 = f32[384]{0:T(512)S(1)} custom-call(bf16[384,768]{1,0:T(8,128)(2,1)} %emb.1, s32[384]{0:T(512)} %order.1), custom_call_target="tpu_custom_call" | custom-call | tf_op jit(solution)/shard_map/pallas_call | solution.py:617
  34.1 0.6 %copy.4 = f32[384]{0:T(512)} copy(f32[384]{0:T(512)S(1)} %shard_map.28) | data formatting | bytes 3072

commit v3 on v2

--- a/solution.py
+++ b/solution.py
@@ -50,6 +50,8 @@
     own = lay.slots
     last = S - 1
     rows_here = n // chunks
+    early = (chunks + 1) // 2 if lay.hold else chunks
+    half = early * rows_here
     align = PIECE if rows_here % PIECE == 0 else rows_here
     r, c = lax.axis_index("row"), lax.axis_index("col")
     z, f = r // F, lax.rem(r, F)
@@ -83,9 +85,14 @@
 
     pairs = [(k, min(2, chunks - k)) for k in range(0, chunks, 2)]
 
+    group_sizes = (1, len(lay.near), len(lay.far))
+
+    def kind(i):
+        return 0 if i < 0 else 1 if i in lay.near else 2
+
     def plane_copy(i, k):
         part = units.at[span(slot, k)]
-        return remote(part, part, ps, pr.at[i, k], plane_id(*lay.offsets[i], 0))
+        return remote(part, part, ps, pr.at[i, k // 2], plane_id(*lay.offsets[i], 0))
 
     def relay_copy(i, k):
         df, dx = lay.offsets[i]
@@ -96,21 +103,20 @@
     def sibling_copy(i, k, count):
         src = chip if i < 0 else source_chip(*lay.offsets[i])
         part = units.at[span(src * C + core, k, count)]
-        return remote(part, part, ps, sr.at[i + 1], plane_id(0, 0, 1))
-
-    def near_wait(i, k):
+        return remote(part, part, ps, sr.at[kind(i)], plane_id(0, 0, 1))
+
+    def near_wait(i, g):
         src = source_chip(*lay.offsets[i]) * C + core
-        here(units.at[span(src, k)], pr.at[i, k]).wait_recv()
+        here(units.at[span(src, *pairs[g])], pr.at[i, g]).wait_recv()
 
     def far_wait(i, g):
         src = source_chip(*lay.offsets[i]) * C + core
         k, count = pairs[g]
         here(units.at[span(src, k, count)], fr.at[i - len(lay.near), g]).wait_recv()
 
-    def sibling_wait(i):
-        src = chip if i < 0 else source_chip(*lay.offsets[i])
-        part = units.at[span(src * C + lax.rem(core + 1, C), 0, chunks)]
-        here(part, sr.at[i + 1]).wait_recv()
+    def sibling_wait(which):
+        count = group_sizes[which]
+        here(units.at[pl.ds(0, count * n)], sr.at[which]).wait_recv()
 
     sends_up = z < last
     sends_down = z == last
@@ -132,10 +138,13 @@
     def goes_on(w):
         return (z >= w) & (z < last - 1)
 
+    def lr_at(w, k):
+        return lr.at[w, 0] if w > 1 and w == last - 1 else lr.at[w, k]
+
     def line_copy(src, k, dst_slot, tag, there):
         return remote(
             src, line.at[dst_slot, pl.ds(k * rows_here, rows_here)],
-            ls.at[tag], lr.at[dst_slot, k], line_id(there),
+            ls.at[tag], lr_at(dst_slot, k), line_id(there),
         )
 
     def own_part(k):
@@ -147,6 +156,17 @@
     def own_up(k):
         return line_copy(own_part(k), k, 1, 0, z + 1)
 
+    held_back = list(range(early, chunks))
+    tail_lead = [(0, k) for k in held_back[1:2] if C > 1] + [(C - 1, k) for k in held_back]
+    tail_rest = [(0, k) for k in held_back if k not in held_back[1:2]] if C > 1 else []
+
+    def tail_up(which, k):
+        part = units.at[span(chip * C + which, k)]
+        where = {"row": (z + 1) * F + f, "col": x * C + which}
+        return remote(
+            part, line.at[1, pl.ds(k * rows_here, rows_here)], ls.at[S - 1], lr.at[1, k], where
+        )
+
     def own_down(k):
         return line_copy(own_part(k), k, 0, 0, z - 2)
 
@@ -157,7 +177,7 @@
         return line_copy(slot_part(0, k), k, 0, 1, z - 1)
 
     def line_wait(w, k):
-        here(slot_part(w, k), lr.at[w, k]).wait_recv()
+        here(slot_part(w, k), lr_at(w, k)).wait_recv()
 
     def line_order(src, dst_slot, tag, there):
         return remote(src, line_orders.at[dst_slot], los.at[tag], lor.at[dst_slot], line_id(there))
@@ -178,23 +198,21 @@
         return remote(orders.at[src], orders.at[src], os_, sem, where)
 
     def order_copy(i):
-        return order_send(slot, or_.at[i], plane_id(*lay.offsets[i], 0))
+        return order_send(slot, or_.at[0], plane_id(*lay.offsets[i], 0))
 
     def order_relay(i):
         df, dx = lay.offsets[i]
-        return order_send(source_chip(0, dx) * C + core, or_.at[i], plane_id(df, 0, 0))
-
-    def order_wait(i):
-        src = source_chip(*lay.offsets[i]) * C + core
-        here(orders.at[src], or_.at[i]).wait_recv()
+        return order_send(source_chip(0, dx) * C + core, or_.at[1], plane_id(df, 0, 0))
+
+    def order_wait(which):
+        here(orders.at[pl.ds(0, group_sizes[which])], or_.at[which - 1]).wait_recv()
 
     def order_across(i):
         src = chip if i < 0 else source_chip(*lay.offsets[i])
-        return order_send(src * C + core, osr.at[i + 1], plane_id(0, 0, 1))
-
-    def order_across_wait(i):
-        src = chip if i < 0 else source_chip(*lay.offsets[i])
-        here(orders.at[src * C + lax.rem(core + 1, C)], osr.at[i + 1]).wait_recv()
+        return order_send(src * C + core, osr.at[kind(i)], plane_id(0, 0, 1))
+
+    def order_across_wait(which):
+        here(orders.at[pl.ds(0, group_sizes[which])], osr.at[which]).wait_recv()
 
     barrier = pltpu.get_barrier_semaphore()
     steps = [(*lay.offsets[i], 0) for i in lay.near] + ([(0, 0, 1)] if C > 1 else [])
@@ -207,24 +225,25 @@
                 barrier, inc=1, device_id=line_id(which), device_id_type=MESH
             )
         )
-    loads = [
-        pltpu.make_async_copy(emb, raw, load.at[0]),
-        pltpu.make_async_copy(order, own_order, load.at[1]),
-    ]
+    loads = [pltpu.make_async_copy(order, own_order, load.at[0])]
+    for at, count in ((0, half), (half, n - half)):
+        if count:
+            rows = pl.ds(at, count)
+            loads.append(pltpu.make_async_copy(emb.at[rows], raw.at[rows], load.at[len(loads)]))
     for one in loads:
         one.start()
     row_best[...] = jnp.full(row_best.shape, -1.0, jnp.float32)
     col_best[...] = jnp.full(col_best.shape, -1.0, jnp.float32)
+    loads[0].wait()
+    orders[pl.ds(slot, 1)] = own_order[...].reshape(1, 1, n)
     loads[1].wait()
-    orders[pl.ds(slot, 1)] = own_order[...].reshape(1, 1, n)
-    loads[0].wait()
 
     def normalize(k):
         floats = raw[pl.ds(k * rows_here, rows_here), :].astype(jnp.float32)
         scale = lax.rsqrt(jnp.sum(floats * floats, axis=1, keepdims=True) + 1e-06)
         units[span(slot, k), :] = (floats * scale).astype(jnp.bfloat16)
 
-    for k in range(chunks):
+    for k in range(early):
         normalize(k)
     lines = jnp.minimum(z, 1) + jnp.minimum(last - z, 1)
     if lay.down:
@@ -237,10 +256,15 @@
             for one in copies:
                 one().start()
 
-    early = (chunks + 2) // 3 if lay.hold else chunks
     holds = z == 1 if lay.hold else z < 0
+    lead = core == C - 1
     if S > 1:
         start(sends_up, order_up, *[functools.partial(own_up, k) for k in range(early)])
+    if half < n:
+        loads[2].wait()
+        for k in range(early, chunks):
+            normalize(k)
+    if half < n and S > 1:
         start(sends_up & jnp.logical_not(holds),
               *[functools.partial(own_up, k) for k in range(early, chunks)])
     if lay.down:
@@ -354,9 +378,10 @@
         def run():
             lax.fori_loop(0, lay.chips // wide, body, 0)
 
-    for i in lay.near:
-        order_wait(i)
-        if C > 1:
+    if lay.near:
+        order_wait(1)
+    if C > 1:
+        for i in lay.near:
             order_across(i).start()
     for i in lay.far:
         order_relay(i).start()
@@ -374,12 +399,11 @@
     if S > 1:
         take_order(1, valid(1))
     if C > 1:
-        order_across_wait(-1)
-        sibling_wait(-1)
+        order_across_wait(0)
+        sibling_wait(0)
     own_item(chip)
     held = z == 2 if lay.hold else z < 0
     straight = jnp.logical_not(held)
-    half = early * rows_here
 
     def take(w, k, cond):
         @pl.when(cond)
@@ -405,14 +429,15 @@
             if C > 1:
                 sibling_copy(i, *pairs[g]).start()
 
-    def near_chunk(k):
+    def near_group(g):
         for i in lay.near:
-            near_wait(i, k)
-        for i in lay.far:
-            relay_copy(i, k).start()
+            near_wait(i, g)
+        for k in range(pairs[g][0], sum(pairs[g])):
+            for i in lay.far:
+                relay_copy(i, k).start()
         if C > 1:
             for i in lay.near:
-                sibling_copy(i, k, 1).start()
+                sibling_copy(i, *pairs[g]).start()
 
     for p in range(chunks + 2 * max(S - 4, 0) + 1):
         if p < chunks and S > 1:
@@ -424,20 +449,23 @@
             if 0 <= k < chunks:
                 take(w, k, goes_on(w))
         if lay.hold and p == chunks - 1:
-            start(holds, *[functools.partial(own_up, k) for k in range(early, chunks)])
+            start(holds & lead, *[functools.partial(tail_up, *one) for one in tail_lead])
+            if tail_rest:
+                start(holds & (core == 0), *[functools.partial(tail_up, *one) for one in tail_rest])
         take_down(p)
-        if p < chunks:
-            near_chunk(p)
+        if p < chunks and (p % 2 or p == chunks - 1):
+            near_group(p // 2)
         if lay.hold and p == early + 1:
             line_sweep(1, "self", 0, half, held)
     if C > 1:
-        for i in lay.near:
-            order_across_wait(i)
-            sibling_wait(i)
+        if lay.near:
+            order_across_wait(1)
+            sibling_wait(1)
     sweep_own("near")
-    for i in lay.far:
-        order_wait(i)
-        if C > 1:
+    if lay.far:
+        order_wait(2)
+    if C > 1:
+        for i in lay.far:
             order_across(i).start()
     far_group(0)
     ends = z == last - 1
@@ -455,8 +483,11 @@
     def take_rows(w, cond):
         @pl.when(valid(w) & cond)
         def run():
-            for k in range(chunks):
-                line_wait(w, k)
+            if w > 1 and w == last - 1:
+                here(line.at[w], lr_at(w, 0)).wait_recv()
+            else:
+                for k in range(chunks):
+                    line_wait(w, k)
         take_order(w, valid(w) & cond)
 
     if S > 1:
@@ -470,29 +501,32 @@
         line_sweep(w, "self", 0, n, z < last)
     for g in range(1, len(pairs) - 1):
         far_group(g)
+    if lay.down:
+        take_rows(0, bottom)
+        line_sweep(0, "self", 0, n, bottom)
+    for g in range(max(len(pairs) - 1, 1), len(pairs)):
+        far_group(g)
     if S > 1:
         line_sweep(1, "near", 0, n, straight)
     for w in range(2, last):
         line_sweep(w, "near", 0, n, z < last)
-    for g in range(max(len(pairs) - 1, 1), len(pairs)):
-        far_group(g)
     if lay.down:
-        line_sweep(0, "near", 0, n, relays_down)
+        line_sweep(0, "near", 0, n, valid(0))
     if C > 1:
-        for i in lay.far:
-            order_across_wait(i)
-            sibling_wait(i)
+        if lay.far:
+            order_across_wait(2)
+            sibling_wait(2)
     if lay.hold:
         pl.when(held)(lambda: sweep("far", [(own, 0, n), (2, 0, n), (1, 0, half)]))
         pl.when(z == 1)(lambda: sweep("far", [(own, 0, n), (0, 0, n), (1, 0, n)]))
         pl.when(z == last)(lambda: sweep("far", [(own, 0, n), (1, 0, n)]))
-        pl.when(bottom)(lambda: sweep_own("far"))
+        pl.when(bottom)(lambda: sweep("far", [(own, 0, n), (0, 0, n)]))
     else:
         sweep_own("far")
         for w in range(2, last):
             line_sweep(w, "far", 0, n, z < last)
         if lay.down:
-            line_sweep(0, "far", 0, n, relays_down)
+            line_sweep(0, "far", 0, n, valid(0))
         if S > 1:
             line_sweep(1, "far", 0, n, straight)
     for w in range(2, last):
@@ -500,22 +534,21 @@
     if S > 1:
         give_back(1, straight)
     if lay.down:
-        give_back(0, relays_down)
-        take_rows(0, bottom)
-        wide_sweep(0, 0, n, bottom)
-        give_back(0, bottom)
-    final = (chunks - 1) * rows_here
+        give_back(0, valid(0))
+    kept = early
+    final = kept * rows_here
     tail = final // LANES * LANES
     if lay.hold:
-        for k in range(early, chunks - 1):
+        for k in range(early, kept):
             take(1, k, held)
-        if chunks - 1 > early:
+        if kept > early:
             wide_sweep(1, half, final - half, held)
         if tail:
             @pl.when(held)
             def run():
                 line_res[1, :, :tail] = jnp.max(row_best[1, :tail, :].T, axis=0, keepdims=True)
-        take(1, chunks - 1, held)
+        for k in range(kept, chunks):
+            take(1, k, held)
 
     def result_copy(df, dx, dc):
         there = (lax.rem(f + df, F) * X + lax.rem(x + dx, X)) * C + lax.rem(core + dc, C)
@@ -598,7 +631,21 @@
             sent(line_orders.at[0], los.at[tag])
 
     if S > 1:
-        line_sent((sends_up | sends_down) if lay.down else sends_up, 0)
+        whole = ((sends_up | sends_down) if lay.down else sends_up) & jnp.logical_not(holds)
+        line_sent(whole, 0)
+    if lay.hold:
+        @pl.when(holds)
+        def run():
+            sent(line.at[0, pl.ds(0, half)], ls.at[0])
+            sent(line_orders.at[0], los.at[0])
+
+        def tail_sent(cond, pieces):
+            if pieces:
+                part = units.at[pl.ds(0, len(pieces) * rows_here)]
+                pl.when(holds & cond)(lambda: sent(part, ls.at[S - 1]))
+
+        tail_sent(lead, tail_lead)
+        tail_sent(core == 0, tail_rest)
     if lay.down:
         line_sent(relays_down, 1)
     for w in range(1, last - 1):
@@ -633,11 +680,11 @@
             vmem((lay.slots, 1, n), jnp.float32),
             vmem((lay.plane, 1, n), jnp.float32),
             vmem((S, 1, n), jnp.float32),
-            dma((2,)),
-            dma(()), dma((near, chunks)), dma((far, (chunks + 1) // 2)), dma((near + far + 1,)),
+            dma((3,)),
+            dma(()), dma((near, (chunks + 1) // 2)), dma((far, (chunks + 1) // 2)), dma((3,)),
             dma((S,)), dma((lay.slots, chunks)),
-            dma(()), dma((near + far,)), dma((near + far + 1,)),
-            dma((S,)), dma((lay.slots,)),
+            dma(()), dma((2,)), dma((3,)),
+            dma((max(S - 1, 1),)), dma((lay.slots,)),
             dma(()), dma(()),
             dma((lay.slots,)), dma((S,)),
         ],

time: 34.9 us -> 33.4 us (0.957)
  Pallas kernels: 34.1 us -> 32.4 us
    pallas_call x1, Pallas kernels: 34.1 us -> 32.4 us  [shards(): pl.pallas_call(functools.partial(kernel, lay, n, chunks), out_shape=vmem(...]
where the time goes in v3:
time: 33.4 us; the launch traced here: 33 us
  Pallas kernels  32.4 us (97%)
  local copies, waits for them, and re-layouts  0.58 us (2%)
    pallas_call x1, Pallas kernels, shards(): pl.pallas_call(functools.partial(kernel, lay, n, chunks), out_shape=vmem(...  32.4 us

profile of v3, /device:TPU:17, one launch (start us, length us, event | category | flops | bytes accessed | tf_op | source)
XLA Modules:
  0.0 33.0 jit_solution(14793993877589867503)
XLA Ops:
  0.0 32.4 %shard_map.28 = f32[384]{0:T(512)S(1)} custom-call(bf16[384,768]{1,0:T(8,128)(2,1)} %emb.1, s32[384]{0:T(512)} %order.1), custom_call_target="tpu_custom_call" | custom-call | tf_op jit(solution)/shard_map/pallas_call | solution.py:664
  32.4 0.6 %copy.4 = f32[384]{0:T(512)} copy(f32[384]{0:T(512)S(1)} %shard_map.28) | data formatting | bytes 3072

commit v4 on v3

--- a/solution.py
+++ b/solution.py
@@ -43,7 +43,7 @@
     lay, n, chunks,
     emb, order, out,
     raw, own_order, units, line, orders, line_orders, col_orders,
-    row_best, col_best, plane_res, line_res, plane_in, line_in,
+    sums, row_best, col_best, plane_res, line_res, plane_in, line_in,
     load, ps, pr, fr, sr, ls, lr, os_, or_, osr, los, lor, rs, rr, lrs, lrr,
 ):
     S, F, X, C = lay.slow, lay.fast, lay.xs, lay.cores
@@ -92,27 +92,26 @@
 
     def plane_copy(i, k):
         part = units.at[span(slot, k)]
-        return remote(part, part, ps, pr.at[i, k // 2], plane_id(*lay.offsets[i], 0))
+        return remote(part, part, ps, pr.at[k // 2], plane_id(*lay.offsets[i], 0))
 
     def relay_copy(i, k):
         df, dx = lay.offsets[i]
         src, step = ((0, dx), (df, 0)) if k % 2 == 0 else ((df, 0), (0, dx))
         part = units.at[span(source_chip(*src) * C + core, k)]
-        return remote(part, part, ps, fr.at[i - len(lay.near), k // 2], plane_id(*step, 0))
+        return remote(part, part, ps, fr.at[k // 2], plane_id(*step, 0))
 
     def sibling_copy(i, k, count):
         src = chip if i < 0 else source_chip(*lay.offsets[i])
         part = units.at[span(src * C + core, k, count)]
         return remote(part, part, ps, sr.at[kind(i)], plane_id(0, 0, 1))
 
-    def near_wait(i, g):
-        src = source_chip(*lay.offsets[i]) * C + core
-        here(units.at[span(src, *pairs[g])], pr.at[i, g]).wait_recv()
-
-    def far_wait(i, g):
-        src = source_chip(*lay.offsets[i]) * C + core
-        k, count = pairs[g]
-        here(units.at[span(src, k, count)], fr.at[i - len(lay.near), g]).wait_recv()
+    def near_wait(g):
+        part = units.at[pl.ds(0, len(lay.near) * pairs[g][1] * rows_here)]
+        here(part, pr.at[g]).wait_recv()
+
+    def far_wait(g):
+        part = units.at[pl.ds(0, len(lay.far) * pairs[g][1] * rows_here)]
+        here(part, fr.at[g]).wait_recv()
 
     def sibling_wait(which):
         count = group_sizes[which]
@@ -122,29 +121,38 @@
     sends_down = z == last
     relays_down = (z > 0) & (z < last - 1)
 
-    def meets(src, dst):
-        found = ((src < dst) & (dst < last)) | ((src == last - 1) & (dst == last))
-        return found | ((src == last) & (dst < last - 1)) if lay.down else found
-
     def source(w):
         return last if w == 0 else z - w
 
-    def valid(w):
+    def valid(w, z=z):
         if w == 0:
-            return z < last - 1
+            return (z < last - 1) & lay.down
         found = (z >= w) & (z < last)
         return (found | (z == last)) if w == 1 else found
 
-    def goes_on(w):
+    def goes_on(w, z=z):
         return (z >= w) & (z < last - 1)
 
+    def results_of(src):
+        return [(src + w, w) for w in range(1, lay.slots) if src + w < S and valid(w, src + w)] + [
+            (there, 0) for there in range(S - 2) if src == last
+        ]
+
+    def place_of(w):
+        found = jnp.int32(0)
+        for there in range(S):
+            if valid(w, there):
+                owner = last if w == 0 else there - w
+                found = jnp.where(z == there, results_of(owner).index((there, w)), found)
+        return found
+
     def lr_at(w, k):
-        return lr.at[w, 0] if w > 1 and w == last - 1 else lr.at[w, k]
-
-    def line_copy(src, k, dst_slot, tag, there):
+        return lr.at[w * chunks + (k if w < 2 or w != last - 1 else 0)]
+
+    def line_copy(src, k, dst_slot, there):
         return remote(
             src, line.at[dst_slot, pl.ds(k * rows_here, rows_here)],
-            ls.at[tag], lr_at(dst_slot, k), line_id(there),
+            ls, lr_at(dst_slot, k), line_id(there),
         )
 
     def own_part(k):
@@ -154,45 +162,54 @@
         return line.at[w, pl.ds(k * rows_here, rows_here)]
 
     def own_up(k):
-        return line_copy(own_part(k), k, 1, 0, z + 1)
+        return line_copy(own_part(k), k, 1, z + 1)
 
     held_back = list(range(early, chunks))
+    depth = units.shape[1]
+    by = len(held_back)
+    cut = depth // by if by and depth % (by * LANES) == 0 else 0
+
+    def held_part(row, k):
+        if cut:
+            return pl.ds(row + half, n - half), pl.ds((k - early) * cut, cut)
+        return pl.ds(row + k * rows_here, rows_here), slice(None)
+
     tail_lead = [(0, k) for k in held_back[1:2] if C > 1] + [(C - 1, k) for k in held_back]
     tail_rest = [(0, k) for k in held_back if k not in held_back[1:2]] if C > 1 else []
 
     def tail_up(which, k):
-        part = units.at[span(chip * C + which, k)]
+        row = pl.multiple_of((chip * C + which) * n, LANES)
         where = {"row": (z + 1) * F + f, "col": x * C + which}
         return remote(
-            part, line.at[1, pl.ds(k * rows_here, rows_here)], ls.at[S - 1], lr.at[1, k], where
+            units.at[held_part(row, k)], line.at[(1, *held_part(0, k))], ls, lr_at(1, k), where
         )
 
     def own_down(k):
-        return line_copy(own_part(k), k, 0, 0, z - 2)
+        return line_copy(own_part(k), k, 0, z - 2)
 
     def relay_up(w, k):
-        return line_copy(slot_part(w, k), k, w + 1, 1 + w, z + 1)
+        return line_copy(slot_part(w, k), k, w + 1, z + 1)
 
     def relay_down(k):
-        return line_copy(slot_part(0, k), k, 0, 1, z - 1)
+        return line_copy(slot_part(0, k), k, 0, z - 1)
 
     def line_wait(w, k):
         here(slot_part(w, k), lr_at(w, k)).wait_recv()
 
-    def line_order(src, dst_slot, tag, there):
-        return remote(src, line_orders.at[dst_slot], los.at[tag], lor.at[dst_slot], line_id(there))
+    def line_order(src, dst_slot, there):
+        return remote(src, line_orders.at[dst_slot], los, lor.at[dst_slot], line_id(there))
 
     def order_up():
-        return line_order(orders.at[slot], 1, 0, z + 1)
+        return line_order(orders.at[slot], 1, z + 1)
 
     def order_down():
-        return line_order(orders.at[slot], 0, 0, z - 2)
+        return line_order(orders.at[slot], 0, z - 2)
 
     def order_on_up(w):
-        return line_order(line_orders.at[w], w + 1, 1 + w, z + 1)
+        return line_order(line_orders.at[w], w + 1, z + 1)
 
     def order_on_down():
-        return line_order(line_orders.at[0], 0, 1, z - 1)
+        return line_order(line_orders.at[0], 0, z - 1)
 
     def order_send(src, sem, where):
         return remote(orders.at[src], orders.at[src], os_, sem, where)
@@ -287,16 +304,17 @@
 
     width = C * n
 
-    def scores(lhs, first_chip, wide=1):
-        rhs = units[pl.ds(pl.multiple_of(first_chip * width, LANES), wide * width), :]
+    def scores(lhs, first_chip, wide=1, depths=slice(None)):
+        at = pl.multiple_of(first_chip * width, LANES)
+        rhs = units[pl.ds(at, wide * width), depths]
         return lax.dot_general(
             lhs, rhs, (((1,), (1,)), ((), ())), preferred_element_type=jnp.float32
         )
 
-    def fold(s, w, first_chip, both, first=0, count=n, wide=1):
+    def fold(s, w, first_chip, both, first=0, count=n):
         mine = col_orders[w, first:first + count, :]
         rows_max = None
-        for j in range(wide * width // LANES):
+        for j in range(s.shape[1] // LANES):
             part = s[:, j * LANES:(j + 1) * LANES]
             which_chip, at = first_chip + j * LANES // width, j * LANES % width
             core_at, lane_at = at // n, at % n
@@ -371,7 +389,7 @@
     def wide_sweep(w, first, count, cond):
         def body(j, carry):
             s = scores(line[w, first:first + count, :], j * wide, wide)
-            fold(s, w, j * wide, True, first, count, wide)
+            fold(s, w, j * wide, True, first, count)
             return carry
 
         @pl.when(valid(w) & cond)
@@ -424,14 +442,15 @@
                     relay_down(k).start()
 
     def far_group(g):
-        for i in lay.far:
-            far_wait(i, g)
-            if C > 1:
+        if lay.far:
+            far_wait(g)
+        if C > 1:
+            for i in lay.far:
                 sibling_copy(i, *pairs[g]).start()
 
     def near_group(g):
-        for i in lay.near:
-            near_wait(i, g)
+        if lay.near:
+            near_wait(g)
         for k in range(pairs[g][0], sum(pairs[g])):
             for i in lay.far:
                 relay_copy(i, k).start()
@@ -472,7 +491,7 @@
     bottom = z == 0
 
     def line_result(w):
-        return remote(line_res.at[w], line_in.at[z], lrs.at[w], lrr.at[z], line_id(source(w)))
+        return remote(line_res.at[w], line_in.at[place_of(w)], lrs, lrr, line_id(source(w)))
 
     def give_back(w, cond):
         @pl.when(valid(w) & cond)
@@ -496,9 +515,6 @@
             line_sweep(1, "near", 0, half, held)
     if lay.down:
         line_sweep(0, "self", 0, n, relays_down)
-    for w in range(2, last):
-        take_rows(w, ends)
-        line_sweep(w, "self", 0, n, z < last)
     for g in range(1, len(pairs) - 1):
         far_group(g)
     if lay.down:
@@ -506,10 +522,13 @@
         line_sweep(0, "self", 0, n, bottom)
     for g in range(max(len(pairs) - 1, 1), len(pairs)):
         far_group(g)
+    for w in range(2, last):
+        take_rows(w, ends)
+        line_sweep(w, "self", 0, n, z < last if not lay.hold else lead)
     if S > 1:
         line_sweep(1, "near", 0, n, straight)
     for w in range(2, last):
-        line_sweep(w, "near", 0, n, z < last)
+        line_sweep(w, "near", 0, n, z < last if not lay.hold else lead)
     if lay.down:
         line_sweep(0, "near", 0, n, valid(0))
     if C > 1:
@@ -517,7 +536,11 @@
             order_across_wait(2)
             sibling_wait(2)
     if lay.hold:
-        pl.when(held)(lambda: sweep("far", [(own, 0, n), (2, 0, n), (1, 0, half)]))
+        line_sweep(2, "far", 0, n, lead)
+        if C > 1:
+            wide_sweep(2, 0, n, core == 0)
+        give_back(2, z < last)
+        pl.when(held)(lambda: sweep("far", [(own, 0, n), (1, 0, half)]))
         pl.when(z == 1)(lambda: sweep("far", [(own, 0, n), (0, 0, n), (1, 0, n)]))
         pl.when(z == last)(lambda: sweep("far", [(own, 0, n), (1, 0, n)]))
         pl.when(bottom)(lambda: sweep("far", [(own, 0, n), (0, 0, n)]))
@@ -529,26 +552,45 @@
             line_sweep(0, "far", 0, n, valid(0))
         if S > 1:
             line_sweep(1, "far", 0, n, straight)
-    for w in range(2, last):
+    for w in range(2, 2 if lay.hold else last):
         give_back(w, z < last)
     if S > 1:
         give_back(1, straight)
     if lay.down:
         give_back(0, valid(0))
-    kept = early
-    final = kept * rows_here
-    tail = final // LANES * LANES
+    tail = half // LANES * LANES
+    rest = slice((by - 1) * cut, None) if cut else slice(None)
+
+    def take_held(k):
+        @pl.when(held)
+        def run():
+            here(line.at[(1, *held_part(0, k))], lr_at(1, k)).wait_recv()
+
+    def places():
+        return [(j // X, j % X) for j in range(lay.chips - 1, -1, -1)]
+
+    def chip_at(df, dx):
+        return lax.rem(f + df, F) * X + lax.rem(x + dx, X)
+
+    def begin_late(first, stop):
+        depths = slice(first * cut, stop * cut)
+        for j, place in enumerate(places()):
+            s = scores(line[1, half:, depths], chip_at(*place), 1, depths)
+            sums[j] = s + sums[j] if first else s
+
     if lay.hold:
-        for k in range(early, kept):
-            take(1, k, held)
-        if kept > early:
-            wide_sweep(1, half, final - half, held)
         if tail:
             @pl.when(held)
             def run():
                 line_res[1, :, :tail] = jnp.max(row_best[1, :tail, :].T, axis=0, keepdims=True)
-        for k in range(kept, chunks):
-            take(1, k, held)
+        ahead = cut and lay.chips <= 4
+        for k in held_back[:-1]:
+            take_held(k)
+            if ahead:
+                pl.when(held & lead)(lambda k=k: begin_late(k - early, k - early + 1))
+        if ahead and C > 1 and by > 1:
+            pl.when(held & (core == 0))(lambda: begin_late(0, by - 1))
+        take_held(held_back[-1])
 
     def result_copy(df, dx, dc):
         there = (lax.rem(f + df, F) * X + lax.rem(x + dx, X)) * C + lax.rem(core + dc, C)
@@ -580,15 +622,21 @@
 
     def finish_late():
         ready = None
-        for j in range(lay.chips - 1, -1, -1):
-            df, dx = j // X, j % X
-            at = lax.rem(f + df, F) * X + lax.rem(x + dx, X)
-            s = scores(line[1, final:, :], at)
+
+        def settle():
+            s, at, place = ready
+            fold(s, 1, at, True, half, n - half)
+            if place != (0, 0):
+                flush_out(*place)
+
+        for j, place in enumerate(places()):
+            s = scores(line[1, half:, rest], chip_at(*place), 1, rest)
+            if cut:
+                s = s + sums[j]
             if ready is not None:
-                fold(*ready[0], 1, ready[1], True, final, n - final)
-                flush_out(*ready[2])
-            ready = (s,), at, (df, dx)
-        fold(*ready[0], 1, ready[1], True, final, n - final)
+                settle()
+            ready = s, chip_at(*place), place
+        settle()
         line_res[1, :, tail:] = jnp.max(row_best[1, tail:, :].T, axis=0, keepdims=True)
         line_result(1).start()
         flush_out(0, 0, 1)
@@ -597,7 +645,7 @@
         pl.when(held)(finish_late)
         pl.when(straight)(finish)
     elif lay.hold:
-        wide_sweep(1, final, n - final, held)
+        wide_sweep(1, half, n - half, held)
         give_back(1, held)
         finish()
     else:
@@ -608,12 +656,14 @@
         here(plane_in.at[pl.ds(1, lay.plane - 1)], rr).wait_recv()
         best = jnp.maximum(best, jnp.max(plane_in[1:], axis=0))
     plane_res[slot] = best
-    for src in range(S):
-        def gather(src=src):
-            here(line_in.at[src], lrr.at[src]).wait_recv()
-            plane_res[slot] = jnp.maximum(plane_res[slot], line_in[src])
-
-        pl.when(meets(z, jnp.int32(src)))(gather)
+    for there in range(S):
+        count = len(results_of(there))
+        if count:
+            @pl.when(z == there)
+            def run(count=count):
+                part = line_in.at[pl.ds(0, count)]
+                here(part, lrr).wait_recv()
+                plane_res[slot] = jnp.maximum(plane_res[slot], jnp.max(part[...], axis=0))
     out[...] = plane_res[slot].reshape(n)
 
     def sent(part, sem):
@@ -624,42 +674,37 @@
         sent(orders.at[pl.ds(0, lay.plane - 1)], os_)
         sent(plane_in.at[pl.ds(1, lay.plane - 1)], rs)
 
-    def line_sent(cond, tag):
+    def line_sent(cond, pieces, copies, results):
         @pl.when(cond)
         def run():
-            sent(line.at[0], ls.at[tag])
-            sent(line_orders.at[0], los.at[tag])
-
-    if S > 1:
-        whole = ((sends_up | sends_down) if lay.down else sends_up) & jnp.logical_not(holds)
-        line_sent(whole, 0)
-    if lay.hold:
-        @pl.when(holds)
-        def run():
-            sent(line.at[0, pl.ds(0, half)], ls.at[0])
-            sent(line_orders.at[0], los.at[0])
-
-        def tail_sent(cond, pieces):
             if pieces:
-                part = units.at[pl.ds(0, len(pieces) * rows_here)]
-                pl.when(holds & cond)(lambda: sent(part, ls.at[S - 1]))
-
-        tail_sent(lead, tail_lead)
-        tail_sent(core == 0, tail_rest)
-    if lay.down:
-        line_sent(relays_down, 1)
-    for w in range(1, last - 1):
-        line_sent(goes_on(w), 1 + w)
-    for w in range(S):
-        if S > 1 and (w or lay.down):
-            pl.when(valid(w))(lambda w=w: sent(line_res.at[w], lrs.at[w]))
+                sent(units.at[pl.ds(0, pieces * rows_here)], ls)
+            if copies:
+                sent(orders.at[pl.ds(0, copies)], los)
+            if results:
+                sent(plane_in.at[pl.ds(0, results)], lrs)
+
+    for there in range(S):
+        moved = sum(bool(goes_on(w, there)) for w in range(1, last - 1))
+        moved += bool(lay.down and 0 < there < last - 1)
+        owns = there < last or lay.down
+        results = sum(bool(valid(w, there)) for w in range(lay.slots))
+        if S == 1:
+            continue
+        if lay.hold and there == 1:
+            for cond, held_pieces in ((lead, tail_lead), (jnp.logical_not(lead), tail_rest)):
+                pieces = early + moved * chunks + len(held_pieces)
+                line_sent((z == there) & cond, pieces, moved + owns, results)
+        else:
+            line_sent(z == there, (moved + owns) * chunks, moved + owns, results)
 
 
 def shards(lay, embeddings, doc_order):
     n, depth = embeddings.shape
     chunks = n // PIECE if n % PIECE == 0 else 1
     dma = pltpu.SemaphoreType.DMA
-    S, near, far = lay.slow, max(len(lay.near), 1), max(len(lay.far), 1)
+    S = lay.slow
+    pieces = chunks * (lay.slots - lay.hold) + lay.hold
     vmem = pltpu.VMEM
     return pl.pallas_call(
         functools.partial(kernel, lay, n, chunks),
@@ -674,6 +719,7 @@
             vmem((lay.plane, 1, n), jnp.int32),
             vmem((lay.slots, 1, n), jnp.int32),
             vmem((lay.slots + 1, n, LANES), jnp.int32),
+            vmem((min(lay.chips, 4), n // 2, lay.cores * n), jnp.float32),
             vmem((lay.slots, n, LANES), jnp.float32),
             vmem((lay.chips, 8, lay.cores * n), jnp.float32),
             vmem((lay.plane, 1, n), jnp.float32),
@@ -681,12 +727,12 @@
             vmem((lay.plane, 1, n), jnp.float32),
             vmem((S, 1, n), jnp.float32),
             dma((3,)),
-            dma(()), dma((near, (chunks + 1) // 2)), dma((far, (chunks + 1) // 2)), dma((3,)),
-            dma((S,)), dma((lay.slots, chunks)),
+            dma(()), dma(((chunks + 1) // 2,)), dma(((chunks + 1) // 2,)), dma((3,)),
+            dma(()), dma((pieces,)),
             dma(()), dma((2,)), dma((3,)),
-            dma((max(S - 1, 1),)), dma((lay.slots,)),
+            dma(()), dma((lay.slots,)),
             dma(()), dma(()),
-            dma((lay.slots,)), dma((S,)),
+            dma(()), dma(()),
         ],
         compiler_params=pltpu.CompilerParams(
             collective_id=0, has_side_effects=True, vmem_limit_bytes=60 * 1024 * 1024

time: 33.4 us -> 33.4 us (level)
  no operation moved by 1% of the time
where the time goes in v4:
time: 33.4 us; the launch traced here: 33.2 us
  Pallas kernels  32.6 us (98%)
  local copies, waits for them, and re-layouts  0.58 us (2%)
    pallas_call x1, Pallas kernels, shards(): pl.pallas_call(functools.partial(kernel, lay, n, chunks), out_shape=vmem(...  32.6 us

profile of v4, /device:TPU:17, one launch (start us, length us, event | category | flops | bytes accessed | tf_op | source)
XLA Modules:
  0.0 33.2 jit_solution(4245352027072088613)
XLA Ops:
  0.0 32.6 %shard_map.28 = f32[384]{0:T(512)S(1)} custom-call(bf16[384,768]{1,0:T(8,128)(2,1)} %emb.1, s32[384]{0:T(512)} %order.1), custom_call_target="tpu_custom_call" | custom-call | tf_op jit(solution)/shard_map/pallas_call | solution.py:709
  32.6 0.6 %copy.4 = f32[384]{0:T(512)} copy(f32[384]{0:T(512)S(1)} %shard_map.28) | data formatting | bytes 3072

commit v5 on v4

--- a/solution.py
+++ b/solution.py
@@ -468,7 +468,6 @@
             if 0 <= k < chunks:
                 take(w, k, goes_on(w))
         if lay.hold and p == chunks - 1:
-            start(holds & lead, *[functools.partial(tail_up, *one) for one in tail_lead])
             if tail_rest:
                 start(holds & (core == 0), *[functools.partial(tail_up, *one) for one in tail_rest])
         take_down(p)
@@ -509,6 +508,8 @@
                     line_wait(w, k)
         take_order(w, valid(w) & cond)
 
+    if lay.hold:
+        start(holds & lead, *[functools.partial(tail_up, *one) for one in tail_lead])
     if S > 1:
         line_sweep(1, "self", 0, n, straight)
         if lay.hold:

time: 33.4 us -> 33.1 us (level)
  no operation moved by 1% of the time
where the time goes in v5:
time: 33.1 us; the launch traced here: 32.9 us
  Pallas kernels  32.3 us (98%)
  local copies, waits for them, and re-layouts  0.58 us (2%)
    pallas_call x1, Pallas kernels, shards(): pl.pallas_call(functools.partial(kernel, lay, n, chunks), out_shape=vmem(...  32.3 us

profile of v5, /device:TPU:17, one launch (start us, length us, event | category | flops | bytes accessed | tf_op | source)
XLA Modules:
  0.0 32.9 jit_solution(894611936255418402)
XLA Ops:
  0.0 32.3 %shard_map.28 = f32[384]{0:T(512)S(1)} custom-call(bf16[384,768]{1,0:T(8,128)(2,1)} %emb.1, s32[384]{0:T(512)} %order.1), custom_call_target="tpu_custom_call" | custom-call | tf_op jit(solution)/shard_map/pallas_call | solution.py:710
  32.3 0.6 %copy.4 = f32[384]{0:T(512)} copy(f32[384]{0:T(512)S(1)} %shard_map.28) | data formatting | bytes 3072

commit v6 on v5

--- a/solution.py
+++ b/solution.py
@@ -652,6 +652,37 @@
     else:
         finish()
 
+    def sent(part, sem):
+        here(part, sem).wait_send()
+
+    if lay.plane > 1:
+        sent(units.at[pl.ds(0, (lay.plane - 1) * n)], ps)
+        sent(orders.at[pl.ds(0, lay.plane - 1)], os_)
+
+    def line_sent(cond, pieces, copies, results):
+        @pl.when(cond)
+        def run():
+            if pieces:
+                sent(units.at[pl.ds(0, pieces * rows_here)], ls)
+            if copies:
+                sent(orders.at[pl.ds(0, copies)], los)
+            if results:
+                sent(plane_in.at[pl.ds(0, results)], lrs)
+
+    for there in range(S):
+        moved = sum(bool(goes_on(w, there)) for w in range(1, last - 1))
+        moved += bool(lay.down and 0 < there < last - 1)
+        owns = there < last or lay.down
+        results = sum(bool(valid(w, there)) for w in range(lay.slots))
+        if S == 1:
+            continue
+        if lay.hold and there == 1:
+            for cond, held_pieces in ((lead, tail_lead), (jnp.logical_not(lead), tail_rest)):
+                pieces = early + moved * chunks + len(held_pieces)
+                line_sent((z == there) & cond, pieces, moved + owns, results)
+        else:
+            line_sent(z == there, (moved + owns) * chunks, moved + owns, results)
+
     best = jnp.maximum(plane_res[slot], jnp.float32(-1.0))
     if lay.plane > 1:
         here(plane_in.at[pl.ds(1, lay.plane - 1)], rr).wait_recv()
@@ -666,38 +697,8 @@
                 here(part, lrr).wait_recv()
                 plane_res[slot] = jnp.maximum(plane_res[slot], jnp.max(part[...], axis=0))
     out[...] = plane_res[slot].reshape(n)
-
-    def sent(part, sem):
-        here(part, sem).wait_send()
-
     if lay.plane > 1:
-        sent(units.at[pl.ds(0, (lay.plane - 1) * n)], ps)
-        sent(orders.at[pl.ds(0, lay.plane - 1)], os_)
         sent(plane_in.at[pl.ds(1, lay.plane - 1)], rs)
-
-    def line_sent(cond, pieces, copies, results):
-        @pl.when(cond)
-        def run():
-            if pieces:
-                sent(units.at[pl.ds(0, pieces * rows_here)], ls)
-            if copies:
-                sent(orders.at[pl.ds(0, copies)], los)
-            if results:
-                sent(plane_in.at[pl.ds(0, results)], lrs)
-
-    for there in range(S):
-        moved = sum(bool(goes_on(w, there)) for w in range(1, last - 1))
-        moved += bool(lay.down and 0 < there < last - 1)
-        owns = there < last or lay.down
-        results = sum(bool(valid(w, there)) for w in range(lay.slots))
-        if S == 1:
-            continue
-        if lay.hold and there == 1:
-            for cond, held_pieces in ((lead, tail_lead), (jnp.logical_not(lead), tail_rest)):
-                pieces = early + moved * chunks + len(held_pieces)
-                line_sent((z == there) & cond, pieces, moved + owns, results)
-        else:
-            line_sent(z == there, (moved + owns) * chunks, moved + owns, results)
 
 
 def shards(lay, embeddings, doc_order):

time: 33.1 us -> 33.1 us (level)
  no operation moved by 1% of the time
where the time goes in v6:
time: 33.1 us; the launch traced here: 32.9 us
  Pallas kernels  32.3 us (98%)
  local copies, waits for them, and re-layouts  0.58 us (2%)
    pallas_call x1, Pallas kernels, shards(): pl.pallas_call(functools.partial(kernel, lay, n, chunks), out_shape=vmem(...  32.3 us

profile of v6, /device:TPU:17, one launch (start us, length us, event | category | flops | bytes accessed | tf_op | source)
XLA Modules:
  0.0 32.9 jit_solution(10802092550476022369)
XLA Ops:
  0.0 32.3 %shard_map.28 = f32[384]{0:T(512)S(1)} custom-call(bf16[384,768]{1,0:T(8,128)(2,1)} %emb.1, s32[384]{0:T(512)} %order.1), custom_call_target="tpu_custom_call" | custom-call | tf_op jit(solution)/shard_map/pallas_call | solution.py:711
  32.3 0.6 %copy.4 = f32[384]{0:T(512)} copy(f32[384]{0:T(512)S(1)} %shard_map.28) | data formatting | bytes 3072
